TPU v7x, 32 devices: a whole 2x2x4 slice. The times are simulated.
32 devices in a mesh: gx: 4 (over y, core), gy: 4 (over z), gz: 2 (over x).
Axes of the slice: x: 2, y: 2, z: 4, core: 2. Of those that a mesh axis runs over, the one named last changes fastest.
Arguments:
- fractions: float32 [3, 4, 8, 4, 128], P(None, 'gx', 'gy', 'gz'), may hold values from 0 to 1
- polarizability: float32 [4, 8, 4, 128], P('gx', 'gy', 'gz'), may hold values from 0.5 to 2
- occupancy: int32 [4, 8, 4, 128], P('gx', 'gy', 'gz'), may hold values 0 or 1
- pair_mask: int32 [4, 8, 4, 27], P('gx', 'gy', 'gz'), may hold values from 0 to 1, as said below
- perm_field: float32 [6, 4, 8, 4, 128], P(None, 'gx', 'gy', 'gz'), may hold values from -6 to 6
- history: float32 [6, 6, 4, 8, 4, 128], P(None, None, 'gx', 'gy', 'gz'), may hold values from -12 to 12
Outputs:
- induced: float32 [6, 4, 8, 4, 128], P(None, 'gx', 'gy', 'gz')
- change: float32 [], replicated
Inputs may be any that keep to these rules, and one draw needn't show every extreme that they name: pair_mask[t, k] equals pair_mask at tile t + offset(k) for the opposite offset 26 - k (periodic); pair_mask[t, 13] (the tile itself) is 1.
All inputs are finite; a program needn't handle non-finite values. No bound on the sum of `occupancy` on one device may be relied on, other than what follows from the above.
Results may differ from a plain program's by a relative error of at most 0.0003.
Values sent between devices are 32-bit elements; how exact they have to be, the bound alone decides.
A program may use at most 64 MiB of HBM per device.

v0:
```python
import functools

import jax
import jax.numpy as jnp
from jax import lax
from jax.experimental import pallas as pl
from jax.experimental.pallas import tpu as pltpu
from jax.sharding import PartitionSpec as P

CELL_EDGE = 10.0
SOFTENING = 0.3
THOLE_DAMP = 0.39
RELAXATION = 0.7
MESH = pl.DeviceIdType.MESH
AXES = ("gx", "gy", "gz")
ROWS = 8
BLOCK = 32
FIELD_BLOCK = 32


def halo_moves(devices, tiles):
    options = []
    for count, n in zip(devices, tiles):
        if count == 2 and n == 2:
            around = [(1, 0, 2, 2)]
        else:
            around = [(1, n - 1, 1, n + 1), (-1, 0, 1, n)]
        options.append([(0, 0, n, 0)] + around)
    return [
        (a, b, c) for a in options[0] for b in options[1] for c in options[2] if (a[0], b[0], c[0]) != (0, 0, 0)
    ]


def row_moves(devices, tiles, row):
    along_x, along_y, along_z = [
        [(0, 0, n, 0)] + [move[axis] for move in halo_moves(devices, tiles) if move[axis][0] != 0]
        for axis, n in enumerate(tiles)
    ]
    n = tiles[1]
    rows = [(0, row, 1, row)]
    if row == n - 1:
        rows.append((1, row, 1, n + 1))
    if row == 0:
        rows.append((-1, row, 1, n))
    along_x, along_z = list(dict.fromkeys(along_x)), list(dict.fromkeys(along_z))
    return [
        (a, b, c) for a in along_x for b in rows for c in along_z if (a[0], b[0], c[0]) != (0, 0, 0)
    ]


def solve_fit(total, past, lane, pair_lane):
    def pick(a, b):
        index = pair_lane[(min(a, b), max(a, b))]
        return jnp.sum(jnp.where(lane == index, total, 0.0), axis=1, keepdims=True)

    diagonal = [pick(a, a) for a in range(past)]
    trace = diagonal[0]
    for value in diagonal[1:]:
        trace = trace + value
    ridge = 0.001 * trace / past + 1.0
    lower, inverse = {}, []
    for j in range(past):
        pivot = diagonal[j] + ridge
        for m in range(j):
            pivot = pivot - lower[j, m] * lower[j, m]
        inverse.append(1.0 / jnp.sqrt(pivot))
        for i in range(j + 1, past):
            value = pick(i, j)
            for m in range(j):
                value = value - lower[i, m] * lower[j, m]
            lower[i, j] = value * inverse[j]
    forward = []
    for i in range(past):
        value = pick(i, past)
        for m in range(i):
            value = value - lower[i, m] * forward[m]
        forward.append(value * inverse[i])
    coeffs = [None] * past
    for i in reversed(range(past)):
        value = forward[i]
        for m in range(i + 1, past):
            value = value - lower[m, i] * coeffs[m]
        coeffs[i] = value * inverse[i]
    return coeffs


def kernel(
    devices,
    frac_in, pol_in, occ_in, mask_in, perm_in, hist_in,
    out_ref, change_ref,
    frac_ref, pol_ref, occ_ref, mask_ref, perm_ref, hist_ref,
    geom, held_one, held_two, past_sets, own, apart, pull, direct, sums, slots_a, slots_b,
    load_sem, send_all, recv_all, send_geom, recv_geom, send_one, recv_one, send_two, recv_two,
):
    tiles = tuple(frac_ref.shape[1:4])
    slots = frac_ref.shape[4]
    steps = hist_ref.shape[0]
    rows = hist_ref.shape[1]
    past = steps - 1
    total_devices = devices[0] * devices[1] * devices[2]
    at = [lax.axis_index(axis) for axis in AXES]
    me = (at[0] * devices[1] + at[1]) * devices[2] + at[2]
    moves = halo_moves(devices, tiles)
    lane = lax.broadcasted_iota(jnp.int32, (1, slots), 1)
    loads = [
        pltpu.make_async_copy(source, target, load_sem.at[number])
        for number, (source, target) in enumerate(
            (
                (hist_in, hist_ref), (occ_in, occ_ref), (frac_in, frac_ref),
                (pol_in, pol_ref), (perm_in, perm_ref), (mask_in, mask_ref),
            )
        )
    ]
    for load in loads:
        load.start()

    def each_other(act):
        def pair(step, carry):
            ahead = (step // devices[1], step % devices[1])
            first = []
            for axis in range(2):
                place = at[axis] + ahead[axis]
                first.append(jnp.where(place >= devices[axis], place - devices[axis], place))
            for shift in range(devices[2] - 1, -1, -1):
                last = at[2] + shift
                last = jnp.where(last >= devices[2], last - devices[2], last)
                if shift == 0:
                    @pl.when(step > 0)
                    def _():
                        act((first[0], first[1], last))
                else:
                    act((first[0], first[1], last))
            return carry

        lax.fori_loop(0, devices[0] * devices[1], pair, 0)

    barrier = pltpu.get_barrier_semaphore()

    each_other(
        lambda device: pl.semaphore_signal(barrier, inc=1, device_id=device, device_id_type=MESH)
    )
    for load in loads:
        load.wait()

    def everyone(index, held):
        def start(device):
            pltpu.make_async_remote_copy(
                src_ref=held.at[pl.ds(me, 1)],
                dst_ref=held.at[pl.ds(me, 1)],
                send_sem=send_all.at[index],
                recv_sem=recv_all.at[index],
                device_id=device,
                device_id_type=MESH,
            ).start()

        each_other(start)

    def everyone_wait(index, held):
        whole = pltpu.make_async_remote_copy(
            src_ref=held.at[pl.ds(0, total_devices - 1)],
            dst_ref=held.at[pl.ds(0, total_devices - 1)],
            send_sem=send_all.at[index],
            recv_sem=recv_all.at[index],
            device_id=(at[0], at[1], (at[2] + 1) % devices[2]),
            device_id_type=MESH,
        )
        whole.wait_send()
        whole.wait_recv()

    def halo(held, send, recv, moves=moves):
        copies = []
        for number, move in enumerate(moves):
            source = tuple(pl.ds(part[1], part[2]) for part in move)
            place = tuple(pl.ds(part[3], part[2]) for part in move)
            target = tuple((at[axis] + move[axis][0] + devices[axis]) % devices[axis] for axis in range(3))
            copies.append(
                pltpu.make_async_remote_copy(
                    src_ref=held.at[source],
                    dst_ref=held.at[place],
                    send_sem=send.at[number],
                    recv_sem=recv.at[number],
                    device_id=target,
                    device_id_type=MESH,
                )
            )
        return copies

    places = [(x, y, z) for x in range(tiles[0]) for y in range(tiles[1]) for z in range(tiles[2])]
    zero_row = jnp.zeros((1, slots), jnp.float32)
    spare = jnp.zeros((ROWS - rows, slots), jnp.float32)
    filled, scaled, fixed = [], [], []
    for t, (x, y, z) in enumerate(places):
        full = occ_ref[x, y, z, :].reshape(1, slots).astype(jnp.float32)
        pol = pol_ref[x, y, z, :].reshape(1, slots)
        scaled.append(RELAXATION * full * pol)
        tile = jnp.concatenate(
            [frac_ref[c, x, y, z, :].reshape(1, slots) * CELL_EDGE for c in range(3)]
            + [lax.rsqrt(pol)] + [zero_row] * (ROWS - 4),
            axis=0,
        )
        geom[x, y, z] = tile
        for h in range(steps):
            moment = jnp.concatenate(
                [hist_ref[h, c, x, y, z, :].reshape(1, slots) for c in range(rows)], axis=0
            )
            past_sets[h, t] = jnp.concatenate([moment * full, spare], axis=0)
        fixed.append(
            jnp.concatenate(
                [perm_ref[c, x, y, z, :].reshape(1, slots) for c in range(rows)] + [spare], axis=0
            )
        )
    pair_lane = {}
    gram = zero_row
    for a in range(steps):
        for b in range(a, steps):
            product = past_sets[a, 0] * past_sets[b, 0]
            for t in range(1, len(places)):
                product = product + past_sets[a, t] * past_sets[b, t]
            value = jnp.sum(jnp.sum(product, axis=0, keepdims=True), axis=1, keepdims=True)
            pair_lane[(a, b)] = len(pair_lane)
            gram = jnp.where(lane == pair_lane[(a, b)], value, gram)
    slots_a[pl.ds(me, 1)] = gram.reshape(1, 1, slots)

    for t, (x, y, z) in enumerate(places):
        for c in range(4):
            row = geom[x, y, z, c, :].reshape(1, slots)
            own[t, c] = jnp.broadcast_to(row, (slots, slots)).T

    pl.semaphore_wait(barrier, total_devices - 1)
    geom_copies = halo(geom, send_geom, recv_geom)
    everyone(0, slots_a)
    for copy in geom_copies:
        copy.start()

    def clear(step, carry):
        sums[step] = jnp.zeros((rows, slots, slots), jnp.float32)
        return carry

    lax.fori_loop(0, 2 * len(places), clear, 0)
    for move, copy in zip(moves, geom_copies):
        if move[0][0] == 0:
            copy.wait()

    wraps = tuple(n + 2 for n in tiles)

    def wrap(value, size):
        return jnp.where(value < 0, value + size, value)

    def spot(t):
        x = t // (tiles[1] * tiles[2])
        y = t // tiles[2] % tiles[1]
        z = t % tiles[2]
        return (x, y, z)

    def source_rows(held, place, names):
        return [held[place[0], place[1], place[2], pl.ds(c, 1), :] for c in names]

    def geometry(t, nine):
        along_x, along_y = nine // 3 - 1, nine % 3 - 1
        base = spot(t)
        for along_z in (-1, 0, 1):
            along = (along_x, along_y, along_z)
            k = nine * 3 + along_z + 1
            place = tuple(wrap(base[i] + along[i], wraps[i]) for i in range(3))
            source = source_rows(geom, place, range(4))
            source[0] = source[0] + CELL_EDGE * along_x.astype(jnp.float32)
            source[1] = source[1] + CELL_EDGE * along_y.astype(jnp.float32)
            source[2] = source[2] + CELL_EDGE * along_z
            damp = source[3] * THOLE_DAMP
            allowed = mask_ref[base[0], base[1], base[2], k].astype(jnp.float32)
            for first in range(0, slots, BLOCK):
                part = pl.ds(first, BLOCK)
                dx = source[0] - own[t, 0, part, :]
                dy = source[1] - own[t, 1, part, :]
                dz = source[2] - own[t, 2, part, :]
                square = dx * dx + dy * dy + dz * dz + SOFTENING
                root = lax.rsqrt(square)
                root_two = root * root
                cube = root_two * root * allowed
                arg = (square * square) * root * (damp * own[t, 3, part, :])
                fade = jnp.exp(-arg)
                three = 1.0 - fade
                five = three - arg * fade
                direct[t, k, part, :] = three * cube
                radial = five * cube * (3.0 * root_two)
                for i, d in enumerate((dx, dy, dz)):
                    apart[i, t, k, part, :] = d
                    pull[i, t, k, part, :] = radial * d

    count = len(places)

    def same_x(step, carry):
        geometry(step // 3, 3 + step % 3)
        return carry

    def other_x(step, carry):
        part = step % 6
        geometry(step // 6, jnp.where(part < 3, part, part + 3))
        return carry

    lax.fori_loop(0, count * 3, same_x, 0)

    everyone_wait(0, slots_a)
    total = jnp.sum(slots_a[...], axis=0)
    coeffs = solve_fit(total, past, lane, pair_lane)
    for t, (x, y, z) in enumerate(places):
        value = coeffs[0] * past_sets[1, t]
        for h in range(1, past):
            value = value + coeffs[h] * past_sets[h + 1, t]
        held_one[x, y, z] = value
    one_copies = halo(held_one, send_one, recv_one)
    for copy in one_copies:
        copy.start()
    for move, copy in zip(moves, geom_copies):
        if move[0][0] != 0:
            copy.wait()
    lax.fori_loop(0, count * 6, other_x, 0)
    off_diagonal = lax.broadcasted_iota(jnp.int32, (slots, slots), 0) != lax.broadcasted_iota(
        jnp.int32, (slots, slots), 1
    )
    for t in range(count):
        direct[t, 13] = jnp.where(off_diagonal, direct[t, 13], 0.0)

    blocks = slots // FIELD_BLOCK

    def add_sources(held, index, step, base, along_y):
        part = pl.ds(pl.multiple_of(step % blocks * FIELD_BLOCK, FIELD_BLOCK), FIELD_BLOCK)
        t = (base[0] * tiles[1] + base[1]) * tiles[2] + base[2]
        place_y = wrap(base[1] + along_y, wraps[1])

        def plane(along_x, acc):
            acc = list(acc)
            place_x = wrap(base[0] + along_x, wraps[0])
            for along_z in (-1, 0, 1):
                place = (place_x, place_y, wrap(base[2] + along_z, wraps[2]))
                moment = source_rows(held, place, range(rows))
                k = 9 * (along_x + 1) + 3 * (along_y + 1) + along_z + 1
                d = direct[t, k, part, :]
                away = [apart[i, t, k, part, :] for i in range(3)]
                drawn = [pull[i, t, k, part, :] for i in range(3)]
                for s in range(rows // 3):
                    m = moment[3 * s : 3 * s + 3]
                    project = away[0] * m[0] + away[1] * m[1] + away[2] * m[2]
                    for i in range(3):
                        acc[3 * s + i] = acc[3 * s + i] + (project * drawn[i] - d * m[i])
            return tuple(acc)

        acc = lax.fori_loop(
            -1, 2, plane, tuple(sums[index * count + t, c, part, :] for c in range(rows))
        )
        for c in range(rows):
            sums[index * count + t, c, part, :] = acc[c]

    flat = tiles[0] * tiles[2] * blocks

    def to_row(held, index, row):
        def one(step, carry):
            column = step // blocks % (tiles[0] * tiles[2])
            base = (column // tiles[2], row, column % tiles[2])
            add_sources(held, index, step, base, step // flat - 1)
            return carry

        lax.fori_loop(0, 3 * flat, one, 0)

    def from_row(held, index, row):
        def one(step, carry):
            column = step // blocks % (tiles[0] * tiles[2])
            along_y = step // flat - 1
            base = (column // tiles[2], (row - along_y + tiles[1]) % tiles[1], column % tiles[2])
            add_sources(held, index, step, base, along_y)
            return carry

        lax.fori_loop(0, 3 * flat, one, 0)

    square_lane = lax.broadcasted_iota(jnp.int32, (slots, slots), 1)

    def field_of(index, t):
        columns = jnp.zeros((slots, slots), jnp.float32)
        for c in range(rows):
            value = jnp.sum(sums[index * count + t, c], axis=1, keepdims=True)
            columns = jnp.where(square_lane == c, value, columns)
        return columns.T[0:ROWS]

    for copy in one_copies:
        copy.wait()
    two_copies = []
    for row in range(tiles[1]):
        to_row(held_one, 0, row)
        for t, (x, y, z) in enumerate(places):
            if y == row:
                held_two[x, y, z] = (1.0 - RELAXATION) * held_one[x, y, z] + scaled[t] * (
                    fixed[t] + field_of(0, t)
                )
        copies = halo(held_two, send_two.at[row], recv_two.at[row], row_moves(devices, tiles, row))
        for copy in copies:
            copy.start()
        two_copies.append(copies)
    for row in range(tiles[1]):
        for copy in two_copies[row]:
            copy.wait()
        from_row(held_two, 1, row)
    fields = [field_of(1, t) for t in range(count)]
    changed = jnp.zeros((ROWS, slots), jnp.float32)
    size = jnp.zeros((ROWS, slots), jnp.float32)
    for t, (x, y, z) in enumerate(places):
        before = held_two[x, y, z]
        after = (1.0 - RELAXATION) * before + scaled[t] * (fixed[t] + fields[t])
        for c in range(rows):
            out_ref[c, x, y, z, :] = after[c]
        changed = changed + (after - before) * (after - before)
        size = size + after * after

    def all_of(value):
        return jnp.sum(jnp.sum(value, axis=0, keepdims=True), axis=1, keepdims=True)

    pair = jnp.where(lane == 0, all_of(changed), jnp.where(lane == 1, all_of(size), 0.0))
    slots_b[pl.ds(me, 1)] = pair.reshape(1, 1, slots)
    everyone(1, slots_b)
    everyone_wait(1, slots_b)
    pair = jnp.sum(slots_b[...], axis=0)
    above = jnp.sum(jnp.where(lane == 0, pair, 0.0), axis=1, keepdims=True)
    below = jnp.sum(jnp.where(lane == 1, pair, 0.0), axis=1, keepdims=True)
    change_ref[...] = jnp.broadcast_to(jnp.sqrt(above / (below + 1.0)), (1, slots))


def solution(mesh):
    devices = tuple(mesh.shape[axis] for axis in AXES)
    total_devices = devices[0] * devices[1] * devices[2]

    def on_device(fractions, polarizability, occupancy, pair_mask, perm_field, history):
        tiles = fractions.shape[1:4]
        slots = fractions.shape[4]
        count = tiles[0] * tiles[1] * tiles[2]
        wraps = tuple(n + 2 for n in tiles)
        moves = len(halo_moves(devices, tiles))
        rows = history.shape[1]
        vmem = pl.BlockSpec(memory_space=pltpu.VMEM)
        f32 = jnp.float32
        induced, change = pl.pallas_call(
            functools.partial(kernel, devices),
            out_shape=(
                jax.ShapeDtypeStruct(perm_field.shape, f32),
                jax.ShapeDtypeStruct((1, slots), f32),
            ),
            in_specs=[pl.BlockSpec(memory_space=pltpu.HBM)] * 6,
            out_specs=(vmem, vmem),
            scratch_shapes=[
                pltpu.VMEM(fractions.shape, f32),
                pltpu.VMEM(polarizability.shape, f32),
                pltpu.VMEM(occupancy.shape, jnp.int32),
                pltpu.SMEM(pair_mask.shape, jnp.int32),
                pltpu.VMEM(perm_field.shape, f32),
                pltpu.VMEM(history.shape, f32),
                pltpu.VMEM(wraps + (ROWS, slots), f32),
                pltpu.VMEM(wraps + (ROWS, slots), f32),
                pltpu.VMEM(wraps + (ROWS, slots), f32),
                pltpu.VMEM((history.shape[0], count, ROWS, slots), f32),
                pltpu.VMEM((count, 4, slots, slots), f32),
                pltpu.VMEM((3, count, 27, slots, slots), f32),
                pltpu.VMEM((3, count, 27, slots, slots), f32),
                pltpu.VMEM((count, 27, slots, slots), f32),
                pltpu.VMEM((2 * count, rows, slots, slots), f32),
                pltpu.VMEM((total_devices, 1, slots), f32),
                pltpu.VMEM((total_devices, 1, slots), f32),
                pltpu.SemaphoreType.DMA((6,)),
                pltpu.SemaphoreType.DMA((2,)),
                pltpu.SemaphoreType.DMA((2,)),
            ]
            + [pltpu.SemaphoreType.DMA((moves,))] * 4
            + [pltpu.SemaphoreType.DMA((tiles[1], moves))] * 2,
            compiler_params=pltpu.CompilerParams(
                collective_id=0, has_side_effects=True, vmem_limit_bytes=67043328
            ),
        )(fractions, polarizability, occupancy, pair_mask, perm_field, history)
        return induced, change[0, 0]

    in_specs = (
        P(None, "gx", "gy", "gz", None),
        P("gx", "gy", "gz", None),
        P("gx", "gy", "gz", None),
        P("gx", "gy", "gz", None),
        P(None, "gx", "gy", "gz", None),
        P(None, None, "gx", "gy", "gz", None),
    )
    out_specs = (P(None, "gx", "gy", "gz", None), P())
    return jax.shard_map(
        on_device, mesh=mesh, in_specs=in_specs, out_specs=out_specs, check_vma=False
    )
```

profile of v0, /device:TPU:0, one launch (start us, length us, event | category | flops | bytes accessed | tf_op | source)
XLA Modules:
  0.0 54.2 jit_solution(11962246032578375659)
XLA Ops:
  0.6 51.0 %shard_map.77 = (f32[6,1,2,2,128]{4,3,2,1,0:T(2,128)}, f32[1,128]{1,0:T(1,128)}) custom-call(f32[3,1,2,2,128]{4,3,2,1,0:T(2,128)} %frac_in.1, f32[1,2,2,128]{3,2,1,0:T(2,128)} %pol_in.1, s32[1,2,2,128]{3,2,1,0:T(2,128)} %occ_in.1, s32[1,2,2,27]{3,2,1,0:T(2,128)} %mask_in.1, f32[6,1,2,2,128]{4,3,2,1,0:T(2,128)} %perm_in.1, f32[6,6,1,2,2,128]{5,4,3,2,1,0:T(2,128)} %hist_in.1), custom_call_target="tpu_custom_call" | custom-call | tf_op jit(solution)/shard_map/pallas_call | solution.py:439
  51.7 0.0 copy-start
  51.7 1.3 %copy.10 = f32[6,1,2,2,128]{4,3,2,1,0:T(2,128)} copy(f32[6,1,2,2,128]{4,3,2,1,0:T(2,128)} %get-tuple-element.8) | data formatting | bytes 24576
  53.0 0.0 copy-done
Async XLA Ops:
  51.7 1.3 %copy-start = (f32[1,128]{1,0:T(1,128)S(1)}, f32[1,128]{1,0:T(1,128)}, u32[]{:S(2)}) copy-start(f32[1,128]{1,0:T(1,128)} %get-tuple-element.5) | copy-start | bytes 1540
where the time goes:
time: 54.4 us; the launch traced here: 54.2 us
  Pallas kernels  51 us (94%)
  between operations  1.81 us (3%)
  local copies, waits for them, and re-layouts  1.31 us (2%)
    pallas_call x1, Pallas kernels, on_device(): pl.pallas_call(functools.partial(kernel, devices), out_shape=(jax.ShapeDt...  51 us
    unnamed x3, local copies, waits for them, and re-layouts  1.31 us

commit v1 on v0

--- a/solution.py
+++ b/solution.py
@@ -15,7 +15,7 @@
 AXES = ("gx", "gy", "gz")
 ROWS = 8
 BLOCK = 32
-FIELD_BLOCK = 32
+STREAMS = 4
 
 
 def halo_moves(devices, tiles):
@@ -28,23 +28,6 @@
         options.append([(0, 0, n, 0)] + around)
     return [
         (a, b, c) for a in options[0] for b in options[1] for c in options[2] if (a[0], b[0], c[0]) != (0, 0, 0)
-    ]
-
-
-def row_moves(devices, tiles, row):
-    along_x, along_y, along_z = [
-        [(0, 0, n, 0)] + [move[axis] for move in halo_moves(devices, tiles) if move[axis][0] != 0]
-        for axis, n in enumerate(tiles)
-    ]
-    n = tiles[1]
-    rows = [(0, row, 1, row)]
-    if row == n - 1:
-        rows.append((1, row, 1, n + 1))
-    if row == 0:
-        rows.append((-1, row, 1, n))
-    along_x, along_z = list(dict.fromkeys(along_x)), list(dict.fromkeys(along_z))
-    return [
-        (a, b, c) for a in along_x for b in rows for c in along_z if (a[0], b[0], c[0]) != (0, 0, 0)
     ]
 
 
@@ -89,7 +72,7 @@
     frac_in, pol_in, occ_in, mask_in, perm_in, hist_in,
     out_ref, change_ref,
     frac_ref, pol_ref, occ_ref, mask_ref, perm_ref, hist_ref,
-    geom, held_one, held_two, past_sets, own, apart, pull, direct, sums, slots_a, slots_b,
+    geom, held_one, held_two, past_sets, own, spots, turns, links, weights, scaled, fixed, slots_a, slots_b,
     load_sem, send_all, recv_all, send_geom, recv_geom, send_one, recv_one, send_two, recv_two,
 ):
     tiles = tuple(frac_ref.shape[1:4])
@@ -188,11 +171,10 @@
     places = [(x, y, z) for x in range(tiles[0]) for y in range(tiles[1]) for z in range(tiles[2])]
     zero_row = jnp.zeros((1, slots), jnp.float32)
     spare = jnp.zeros((ROWS - rows, slots), jnp.float32)
-    filled, scaled, fixed = [], [], []
     for t, (x, y, z) in enumerate(places):
         full = occ_ref[x, y, z, :].reshape(1, slots).astype(jnp.float32)
         pol = pol_ref[x, y, z, :].reshape(1, slots)
-        scaled.append(RELAXATION * full * pol)
+        scaled[t] = jnp.broadcast_to(RELAXATION * full * pol, (ROWS, slots))
         tile = jnp.concatenate(
             [frac_ref[c, x, y, z, :].reshape(1, slots) * CELL_EDGE for c in range(3)]
             + [lax.rsqrt(pol)] + [zero_row] * (ROWS - 4),
@@ -204,10 +186,8 @@
                 [hist_ref[h, c, x, y, z, :].reshape(1, slots) for c in range(rows)], axis=0
             )
             past_sets[h, t] = jnp.concatenate([moment * full, spare], axis=0)
-        fixed.append(
-            jnp.concatenate(
-                [perm_ref[c, x, y, z, :].reshape(1, slots) for c in range(rows)] + [spare], axis=0
-            )
+        fixed[t] = jnp.concatenate(
+            [perm_ref[c, x, y, z, :].reshape(1, slots) for c in range(rows)] + [spare], axis=0
         )
     pair_lane = {}
     gram = zero_row
@@ -221,27 +201,21 @@
             gram = jnp.where(lane == pair_lane[(a, b)], value, gram)
     slots_a[pl.ds(me, 1)] = gram.reshape(1, 1, slots)
 
-    for t, (x, y, z) in enumerate(places):
-        for c in range(4):
-            row = geom[x, y, z, c, :].reshape(1, slots)
-            own[t, c] = jnp.broadcast_to(row, (slots, slots)).T
-
     pl.semaphore_wait(barrier, total_devices - 1)
     geom_copies = halo(geom, send_geom, recv_geom)
     everyone(0, slots_a)
     for copy in geom_copies:
         copy.start()
 
-    def clear(step, carry):
-        sums[step] = jnp.zeros((rows, slots, slots), jnp.float32)
-        return carry
-
-    lax.fori_loop(0, 2 * len(places), clear, 0)
     for move, copy in zip(moves, geom_copies):
         if move[0][0] == 0:
             copy.wait()
 
     wraps = tuple(n + 2 for n in tiles)
+    row_of = lax.broadcasted_iota(jnp.int32, (ROWS, slots), 0)
+    count = len(places)
+    offsets = 27
+    kinds = 5
 
     def wrap(value, size):
         return jnp.where(value < 0, value + size, value)
@@ -252,8 +226,35 @@
         z = t % tiles[2]
         return (x, y, z)
 
-    def source_rows(held, place, names):
-        return [held[place[0], place[1], place[2], pl.ds(c, 1), :] for c in names]
+    def settle(place, slot):
+        tile = geom[slot[0], slot[1], slot[2]]
+        shift = jnp.zeros((ROWS, slots), jnp.float32)
+        for axis in range(3):
+            corner = CELL_EDGE * (place[axis].astype(jnp.float32) - 0.5 * tiles[axis])
+            shift = jnp.where(row_of == axis, corner, shift)
+        tile = tile + shift
+        spots[slot[0], slot[1], slot[2]] = tile
+        one = jnp.ones((2, slots), jnp.float32)
+        turns[0, slot[0], slot[1], slot[2]] = jnp.concatenate(
+            [tile[0:3], tile[0:3], jnp.zeros((2, slots), jnp.float32)], axis=0
+        )
+        turns[1, slot[0], slot[1], slot[2]] = jnp.concatenate([one, tile[0:3], tile[0:3]], axis=0)
+
+    def settle_plane(along_x):
+        def one(step, carry):
+            y, z = step // wraps[2] - 1, step % wraps[2] - 1
+            place = (along_x, y, z)
+            settle(place, tuple(wrap(place[i], wraps[i]) for i in range(3)))
+            return carry
+
+        lax.fori_loop(0, wraps[1] * wraps[2], one, 0)
+
+    for x in range(tiles[0]):
+        settle_plane(jnp.int32(x))
+    for t, (x, y, z) in enumerate(places):
+        for c in range(4):
+            row = spots[x, y, z, c, :].reshape(1, slots)
+            own[t, c] = jnp.broadcast_to(row, (slots, slots)).T
 
     def geometry(t, nine):
         along_x, along_y = nine // 3 - 1, nine % 3 - 1
@@ -262,11 +263,8 @@
             along = (along_x, along_y, along_z)
             k = nine * 3 + along_z + 1
             place = tuple(wrap(base[i] + along[i], wraps[i]) for i in range(3))
-            source = source_rows(geom, place, range(4))
-            source[0] = source[0] + CELL_EDGE * along_x.astype(jnp.float32)
-            source[1] = source[1] + CELL_EDGE * along_y.astype(jnp.float32)
-            source[2] = source[2] + CELL_EDGE * along_z
-            damp = source[3] * THOLE_DAMP
+            source = [spots[place[0], place[1], place[2], pl.ds(c, 1), :] for c in range(4)]
+            damp = source[3] * -THOLE_DAMP
             allowed = mask_ref[base[0], base[1], base[2], k].astype(jnp.float32)
             for first in range(0, slots, BLOCK):
                 part = pl.ds(first, BLOCK)
@@ -278,16 +276,16 @@
                 root_two = root * root
                 cube = root_two * root * allowed
                 arg = (square * square) * root * (damp * own[t, 3, part, :])
-                fade = jnp.exp(-arg)
+                fade = jnp.exp(arg)
                 three = 1.0 - fade
-                five = three - arg * fade
-                direct[t, k, part, :] = three * cube
+                five = three + arg * fade
+                direct = three * cube
                 radial = five * cube * (3.0 * root_two)
-                for i, d in enumerate((dx, dy, dz)):
-                    apart[i, t, k, part, :] = d
-                    pull[i, t, k, part, :] = radial * d
-
-    count = len(places)
+                for number, value in ((0, radial), (2, direct)):
+                    high = value.astype(jnp.bfloat16)
+                    low = (value - high.astype(jnp.float32)).astype(jnp.bfloat16)
+                    links[t, number, k, part, :] = high
+                    links[t, number + 1, k, part, :] = low
 
     def same_x(step, carry):
         geometry(step // 3, 3 + step % 3)
@@ -314,101 +312,121 @@
     for move, copy in zip(moves, geom_copies):
         if move[0][0] != 0:
             copy.wait()
+    settle_plane(jnp.int32(-1))
+    settle_plane(jnp.int32(tiles[0]))
     lax.fori_loop(0, count * 6, other_x, 0)
     off_diagonal = lax.broadcasted_iota(jnp.int32, (slots, slots), 0) != lax.broadcasted_iota(
         jnp.int32, (slots, slots), 1
     )
+    empty = jnp.zeros((slots, slots), jnp.bfloat16)
     for t in range(count):
-        direct[t, 13] = jnp.where(off_diagonal, direct[t, 13], 0.0)
-
-    blocks = slots // FIELD_BLOCK
-
-    def add_sources(held, index, step, base, along_y):
-        part = pl.ds(pl.multiple_of(step % blocks * FIELD_BLOCK, FIELD_BLOCK), FIELD_BLOCK)
-        t = (base[0] * tiles[1] + base[1]) * tiles[2] + base[2]
-        place_y = wrap(base[1] + along_y, wraps[1])
-
-        def plane(along_x, acc):
-            acc = list(acc)
-            place_x = wrap(base[0] + along_x, wraps[0])
-            for along_z in (-1, 0, 1):
-                place = (place_x, place_y, wrap(base[2] + along_z, wraps[2]))
-                moment = source_rows(held, place, range(rows))
-                k = 9 * (along_x + 1) + 3 * (along_y + 1) + along_z + 1
-                d = direct[t, k, part, :]
-                away = [apart[i, t, k, part, :] for i in range(3)]
-                drawn = [pull[i, t, k, part, :] for i in range(3)]
-                for s in range(rows // 3):
-                    m = moment[3 * s : 3 * s + 3]
-                    project = away[0] * m[0] + away[1] * m[1] + away[2] * m[2]
-                    for i in range(3):
-                        acc[3 * s + i] = acc[3 * s + i] + (project * drawn[i] - d * m[i])
-            return tuple(acc)
-
-        acc = lax.fori_loop(
-            -1, 2, plane, tuple(sums[index * count + t, c, part, :] for c in range(rows))
+        for number in range(STREAMS):
+            own_link = links[t, number, 13].astype(jnp.float32)
+            links[t, number, 13] = jnp.where(off_diagonal, own_link, 0.0).astype(jnp.bfloat16)
+            links[t, number, offsets] = empty
+    spread = wraps[0] * wraps[1] * wraps[2]
+    weights[spread] = empty
+
+    def weigh(held):
+        def one(step, carry):
+            slot = (step // (wraps[1] * wraps[2]), step // wraps[2] % wraps[1], step % wraps[2])
+            moment = held[slot[0], slot[1], slot[2]]
+            along = moment * turns[0, slot[0], slot[1], slot[2]]
+            first = jnp.sum(jnp.where(row_of < 3, along, 0.0), axis=0, keepdims=True)
+            second = jnp.sum(jnp.where(row_of < 3, 0.0, along), axis=0, keepdims=True)
+            which = jnp.logical_or(row_of == 0, jnp.logical_and(row_of >= 2, row_of < 5))
+            both = jnp.where(which, first, second) * turns[1, slot[0], slot[1], slot[2]]
+            parts = [spots[slot[0], slot[1], slot[2], pl.ds(c, 1), :] * moment for c in range(3)]
+            value = jnp.concatenate(parts + [moment, both], axis=0)
+            high = value.astype(jnp.bfloat16).astype(jnp.float32)
+            rest = value - high
+            middle = rest.astype(jnp.bfloat16).astype(jnp.float32)
+            pad = jnp.zeros((slots - 3 * kinds * ROWS, slots), jnp.float32)
+            weights[step] = jnp.concatenate([high, middle, rest - middle, pad], axis=0).astype(jnp.bfloat16)
+            return carry
+
+        lax.fori_loop(0, spread, one, 0)
+
+    def field_of(t, sums):
+        x, y, z = spot(t)
+        radial = (sums[0:slots] + sums[slots : 2 * slots]).T
+        direct = (sums[2 * slots : 3 * slots] + sums[3 * slots : 4 * slots]).T
+
+        def tile(value, kind):
+            total = value[kind * ROWS : (kind + 1) * ROWS]
+            for level in (1, 2):
+                first = (level * kinds + kind) * ROWS
+                total = total + value[first : first + ROWS]
+            return total
+
+        turn = turns[0, x, y, z]
+        plain = tile(radial, 3)
+        both = tile(radial, 4)
+        inner = []
+        for c in range(3):
+            along = (tile(radial, c) - spots[x, y, z, pl.ds(c, 1), :] * plain) * turn
+            first = jnp.sum(jnp.where(row_of < 3, along, 0.0), axis=0, keepdims=True)
+            second = jnp.sum(jnp.where(row_of < 3, 0.0, along), axis=0, keepdims=True)
+            inner.append((first, second))
+        inner = jnp.concatenate(
+            [inner[c][0] for c in range(3)] + [inner[c][1] for c in range(3)] + [zero_row, zero_row], axis=0
         )
-        for c in range(rows):
-            sums[index * count + t, c, part, :] = acc[c]
-
-    flat = tiles[0] * tiles[2] * blocks
-
-    def to_row(held, index, row):
-        def one(step, carry):
-            column = step // blocks % (tiles[0] * tiles[2])
-            base = (column // tiles[2], row, column % tiles[2])
-            add_sources(held, index, step, base, step // flat - 1)
-            return carry
-
-        lax.fori_loop(0, 3 * flat, one, 0)
-
-    def from_row(held, index, row):
-        def one(step, carry):
-            column = step // blocks % (tiles[0] * tiles[2])
-            along_y = step // flat - 1
-            base = (column // tiles[2], (row - along_y + tiles[1]) % tiles[1], column % tiles[2])
-            add_sources(held, index, step, base, along_y)
-            return carry
-
-        lax.fori_loop(0, 3 * flat, one, 0)
-
-    square_lane = lax.broadcasted_iota(jnp.int32, (slots, slots), 1)
-
-    def field_of(index, t):
-        columns = jnp.zeros((slots, slots), jnp.float32)
-        for c in range(rows):
-            value = jnp.sum(sums[index * count + t, c], axis=1, keepdims=True)
-            columns = jnp.where(square_lane == c, value, columns)
-        return columns.T[0:ROWS]
+        lifted = jnp.concatenate([both[2:8], zero_row, zero_row], axis=0)
+        dots = jnp.where(row_of < 3, both[0:1], both[1:2])
+        return lifted - dots * turn - inner - tile(direct, 3)
+
+    def slot_at(base, k):
+        along = (k // 9 - 1, k // 3 % 3 - 1, k % 3 - 1)
+        slot = [wrap(base[i] + along[i], wraps[i]) for i in range(3)]
+        return (slot[0] * wraps[1] + slot[1]) * wraps[2] + slot[2]
+
+    def field(t):
+        base = spot(t)
+        sums = jnp.zeros((STREAMS * slots, slots), jnp.float32)
+        for pair in range(0, offsets, 2):
+            left = jnp.concatenate(
+                [
+                    jnp.concatenate([links[t, number, pair], links[t, number, pair + 1]], axis=1)
+                    for number in range(STREAMS)
+                ],
+                axis=0,
+            )
+            behind = spread if pair + 1 == offsets else slot_at(base, pair + 1)
+            right = jnp.concatenate([weights[slot_at(base, pair)], weights[behind]], axis=1)
+            sums = sums + lax.dot_general(
+                left, right, (((1,), (1,)), ((), ())), preferred_element_type=jnp.float32
+            )
+        return field_of(t, sums)
 
     for copy in one_copies:
         copy.wait()
-    two_copies = []
-    for row in range(tiles[1]):
-        to_row(held_one, 0, row)
-        for t, (x, y, z) in enumerate(places):
-            if y == row:
-                held_two[x, y, z] = (1.0 - RELAXATION) * held_one[x, y, z] + scaled[t] * (
-                    fixed[t] + field_of(0, t)
-                )
-        copies = halo(held_two, send_two.at[row], recv_two.at[row], row_moves(devices, tiles, row))
-        for copy in copies:
-            copy.start()
-        two_copies.append(copies)
-    for row in range(tiles[1]):
-        for copy in two_copies[row]:
-            copy.wait()
-        from_row(held_two, 1, row)
-    fields = [field_of(1, t) for t in range(count)]
-    changed = jnp.zeros((ROWS, slots), jnp.float32)
-    size = jnp.zeros((ROWS, slots), jnp.float32)
-    for t, (x, y, z) in enumerate(places):
+    weigh(held_one)
+
+    def first_pass(t, carry):
+        x, y, z = spot(t)
+        held_two[x, y, z] = (1.0 - RELAXATION) * held_one[x, y, z] + scaled[t] * (fixed[t] + field(t))
+        return carry
+
+    lax.fori_loop(0, count, first_pass, 0)
+    two_copies = halo(held_two, send_two, recv_two)
+    for copy in two_copies:
+        copy.start()
+    for copy in two_copies:
+        copy.wait()
+    weigh(held_two)
+
+    def second_pass(t, carry):
+        changed, size = carry
+        x, y, z = spot(t)
         before = held_two[x, y, z]
-        after = (1.0 - RELAXATION) * before + scaled[t] * (fixed[t] + fields[t])
+        after = (1.0 - RELAXATION) * before + scaled[t] * (fixed[t] + field(t))
         for c in range(rows):
             out_ref[c, x, y, z, :] = after[c]
         changed = changed + (after - before) * (after - before)
-        size = size + after * after
+        return changed, size + after * after
+
+    nothing = jnp.zeros((ROWS, slots), jnp.float32)
+    changed, size = lax.fori_loop(0, count, second_pass, (nothing, nothing))
 
     def all_of(value):
         return jnp.sum(jnp.sum(value, axis=0, keepdims=True), axis=1, keepdims=True)
@@ -456,18 +474,19 @@
                 pltpu.VMEM(wraps + (ROWS, slots), f32),
                 pltpu.VMEM((history.shape[0], count, ROWS, slots), f32),
                 pltpu.VMEM((count, 4, slots, slots), f32),
-                pltpu.VMEM((3, count, 27, slots, slots), f32),
-                pltpu.VMEM((3, count, 27, slots, slots), f32),
-                pltpu.VMEM((count, 27, slots, slots), f32),
-                pltpu.VMEM((2 * count, rows, slots, slots), f32),
+                pltpu.VMEM(wraps + (ROWS, slots), f32),
+                pltpu.VMEM((2,) + wraps + (ROWS, slots), f32),
+                pltpu.VMEM((count, STREAMS, 28, slots, slots), jnp.bfloat16),
+                pltpu.VMEM((wraps[0] * wraps[1] * wraps[2] + 1, slots, slots), jnp.bfloat16),
+                pltpu.VMEM((count, ROWS, slots), f32),
+                pltpu.VMEM((count, ROWS, slots), f32),
                 pltpu.VMEM((total_devices, 1, slots), f32),
                 pltpu.VMEM((total_devices, 1, slots), f32),
                 pltpu.SemaphoreType.DMA((6,)),
                 pltpu.SemaphoreType.DMA((2,)),
                 pltpu.SemaphoreType.DMA((2,)),
             ]
-            + [pltpu.SemaphoreType.DMA((moves,))] * 4
-            + [pltpu.SemaphoreType.DMA((tiles[1], moves))] * 2,
+            + [pltpu.SemaphoreType.DMA((moves,))] * 6,
             compiler_params=pltpu.CompilerParams(
                 collective_id=0, has_side_effects=True, vmem_limit_bytes=67043328
             ),

time: 54.4 us -> 48 us (0.88)
  Pallas kernels: 51 us -> 44.6 us
    pallas_call x1, Pallas kernels: 51 us -> 44.6 us  [on_device(): pl.pallas_call(functools.partial(kernel, devices), out_shape=(jax.ShapeDt...]
where the time goes in v1:
time: 48 us; the launch traced here: 47.7 us
  Pallas kernels  44.6 us (93%)
  between operations  1.81 us (4%)
  local copies, waits for them, and re-layouts  1.31 us (3%)
    pallas_call x1, Pallas kernels, on_device(): pl.pallas_call(functools.partial(kernel, devices), out_shape=(jax.ShapeDt...  44.6 us
    unnamed x3, local copies, waits for them, and re-layouts  1.31 us

profile of v1, /device:TPU:0, one launch (start us, length us, event | category | flops | bytes accessed | tf_op | source)
XLA Modules:
  0.0 47.7 jit_solution(11968287339628221260)
XLA Ops:
  0.6 44.6 %shard_map.77 = (f32[6,1,2,2,128]{4,3,2,1,0:T(2,128)}, f32[1,128]{1,0:T(1,128)}) custom-call(f32[3,1,2,2,128]{4,3,2,1,0:T(2,128)} %frac_in.1, f32[1,2,2,128]{3,2,1,0:T(2,128)} %pol_in.1, s32[1,2,2,128]{3,2,1,0:T(2,128)} %occ_in.1, s32[1,2,2,27]{3,2,1,0:T(2,128)} %mask_in.1, f32[6,1,2,2,128]{4,3,2,1,0:T(2,128)} %perm_in.1, f32[6,6,1,2,2,128]{5,4,3,2,1,0:T(2,128)} %hist_in.1), custom_call_target="tpu_custom_call" | custom-call | tf_op jit(solution)/shard_map/pallas_call | solution.py:457
  45.3 0.0 copy-start
  45.3 1.3 %copy.10 = f32[6,1,2,2,128]{4,3,2,1,0:T(2,128)} copy(f32[6,1,2,2,128]{4,3,2,1,0:T(2,128)} %get-tuple-element.8) | data formatting | bytes 24576
  46.6 0.0 copy-done
Async XLA Ops:
  45.3 1.3 %copy-start = (f32[1,128]{1,0:T(1,128)S(1)}, f32[1,128]{1,0:T(1,128)}, u32[]{:S(2)}) copy-start(f32[1,128]{1,0:T(1,128)} %get-tuple-element.5) | copy-start | bytes 1540

commit v2 on v1

--- a/solution.py
+++ b/solution.py
@@ -16,6 +16,9 @@
 ROWS = 8
 BLOCK = 32
 STREAMS = 4
+SPREAD = 128
+SPREAD_LOW = 96
+SPREAD_PLAIN = 32
 
 
 def halo_moves(devices, tiles):
@@ -72,7 +75,8 @@
     frac_in, pol_in, occ_in, mask_in, perm_in, hist_in,
     out_ref, change_ref,
     frac_ref, pol_ref, occ_ref, mask_ref, perm_ref, hist_ref,
-    geom, held_one, held_two, past_sets, own, spots, turns, links, weights, scaled, fixed, slots_a, slots_b,
+    geom, held_one, held_two, past_sets, spots, columns, turns, links, weights,
+    partial_main, partial_rest, partial_plain, scaled, fixed, slots_a, slots_b,
     load_sem, send_all, recv_all, send_geom, recv_geom, send_one, recv_one, send_two, recv_two,
 ):
     tiles = tuple(frac_ref.shape[1:4])
@@ -150,7 +154,7 @@
         whole.wait_send()
         whole.wait_recv()
 
-    def halo(held, send, recv, moves=moves):
+    def halo(held, send, recv, depth):
         copies = []
         for number, move in enumerate(moves):
             source = tuple(pl.ds(part[1], part[2]) for part in move)
@@ -158,8 +162,8 @@
             target = tuple((at[axis] + move[axis][0] + devices[axis]) % devices[axis] for axis in range(3))
             copies.append(
                 pltpu.make_async_remote_copy(
-                    src_ref=held.at[source],
-                    dst_ref=held.at[place],
+                    src_ref=held.at[source + (pl.ds(0, depth),)],
+                    dst_ref=held.at[place + (pl.ds(0, depth),)],
                     send_sem=send.at[number],
                     recv_sem=recv.at[number],
                     device_id=target,
@@ -202,101 +206,128 @@
     slots_a[pl.ds(me, 1)] = gram.reshape(1, 1, slots)
 
     pl.semaphore_wait(barrier, total_devices - 1)
-    geom_copies = halo(geom, send_geom, recv_geom)
+    geom_copies = halo(geom, send_geom, recv_geom, 4)
     everyone(0, slots_a)
     for copy in geom_copies:
         copy.start()
 
-    for move, copy in zip(moves, geom_copies):
-        if move[0][0] == 0:
-            copy.wait()
-
     wraps = tuple(n + 2 for n in tiles)
     row_of = lax.broadcasted_iota(jnp.int32, (ROWS, slots), 0)
     count = len(places)
-    offsets = 27
-    kinds = 5
+    wide = tiles[2] * slots
+    levels = list(range(tiles[2])) + [-1, tiles[2]]
 
     def wrap(value, size):
         return jnp.where(value < 0, value + size, value)
-
-    def spot(t):
-        x = t // (tiles[1] * tiles[2])
-        y = t // tiles[2] % tiles[1]
-        z = t % tiles[2]
-        return (x, y, z)
 
     def settle(place, slot):
         tile = geom[slot[0], slot[1], slot[2]]
         shift = jnp.zeros((ROWS, slots), jnp.float32)
         for axis in range(3):
-            corner = CELL_EDGE * (place[axis].astype(jnp.float32) - 0.5 * tiles[axis])
+            corner = CELL_EDGE * (jnp.asarray(place[axis], jnp.float32) - 0.5 * tiles[axis])
             shift = jnp.where(row_of == axis, corner, shift)
         tile = tile + shift
         spots[slot[0], slot[1], slot[2]] = tile
+        columns[slot[0], slot[1], slot[2]] = tile.T
         one = jnp.ones((2, slots), jnp.float32)
         turns[0, slot[0], slot[1], slot[2]] = jnp.concatenate(
             [tile[0:3], tile[0:3], jnp.zeros((2, slots), jnp.float32)], axis=0
         )
         turns[1, slot[0], slot[1], slot[2]] = jnp.concatenate([one, tile[0:3], tile[0:3]], axis=0)
 
-    def settle_plane(along_x):
+    def settle_all(xs, ys, zs):
         def one(step, carry):
-            y, z = step // wraps[2] - 1, step % wraps[2] - 1
-            place = (along_x, y, z)
-            settle(place, tuple(wrap(place[i], wraps[i]) for i in range(3)))
+            x = step + xs[0]
+            for y in ys:
+                for z in zs:
+                    settle((x, y, z), (wrap(x, wraps[0]), y % wraps[1], z % wraps[2]))
             return carry
 
-        lax.fori_loop(0, wraps[1] * wraps[2], one, 0)
-
-    for x in range(tiles[0]):
-        settle_plane(jnp.int32(x))
-    for t, (x, y, z) in enumerate(places):
-        for c in range(4):
-            row = spots[x, y, z, c, :].reshape(1, slots)
-            own[t, c] = jnp.broadcast_to(row, (slots, slots)).T
-
-    def geometry(t, nine):
-        along_x, along_y = nine // 3 - 1, nine % 3 - 1
-        base = spot(t)
-        for along_z in (-1, 0, 1):
-            along = (along_x, along_y, along_z)
-            k = nine * 3 + along_z + 1
-            place = tuple(wrap(base[i] + along[i], wraps[i]) for i in range(3))
-            source = [spots[place[0], place[1], place[2], pl.ds(c, 1), :] for c in range(4)]
-            damp = source[3] * -THOLE_DAMP
-            allowed = mask_ref[base[0], base[1], base[2], k].astype(jnp.float32)
+        lax.fori_loop(0, len(xs), one, 0)
+
+    near_y, far_y = list(range(tiles[1])), [-1, tiles[1]]
+    every_x = list(range(-1, tiles[0] + 1))
+    own_z, side_z = list(range(tiles[2])), [-1, tiles[2]]
+
+    def geometry(x, y, along_x, along_y, zs):
+        nine = (along_x + 1) * 3 + along_y + 1
+        line = x * tiles[1] + y
+        slot_x, slot_y = wrap(x + along_x, wraps[0]), wrap(y + along_y, wraps[1])
+        for level in zs:
+            spot_at = levels.index(level)
+            slot_z = level % wraps[2]
+            takers = [z for z in range(tiles[2]) if abs(level - z) <= 1]
+            fixed_rows = [[spots[x, y, z, pl.ds(c, 1), :] for c in range(4)] for z in takers]
+            allowed = [mask_ref[x, y, z, nine * 3 + level - z + 1].astype(jnp.float32) for z in takers]
+            damps = [own_row[3] * -THOLE_DAMP for own_row in fixed_rows]
             for first in range(0, slots, BLOCK):
                 part = pl.ds(first, BLOCK)
-                dx = source[0] - own[t, 0, part, :]
-                dy = source[1] - own[t, 1, part, :]
-                dz = source[2] - own[t, 2, part, :]
-                square = dx * dx + dy * dy + dz * dz + SOFTENING
-                root = lax.rsqrt(square)
-                root_two = root * root
-                cube = root_two * root * allowed
-                arg = (square * square) * root * (damp * own[t, 3, part, :])
-                fade = jnp.exp(arg)
-                three = 1.0 - fade
-                five = three + arg * fade
-                direct = three * cube
-                radial = five * cube * (3.0 * root_two)
-                for number, value in ((0, radial), (2, direct)):
-                    high = value.astype(jnp.bfloat16)
-                    low = (value - high.astype(jnp.float32)).astype(jnp.bfloat16)
-                    links[t, number, k, part, :] = high
-                    links[t, number + 1, k, part, :] = low
-
-    def same_x(step, carry):
-        geometry(step // 3, 3 + step % 3)
-        return carry
-
-    def other_x(step, carry):
-        part = step % 6
-        geometry(step // 6, jnp.where(part < 3, part, part + 3))
-        return carry
-
-    lax.fori_loop(0, count * 3, same_x, 0)
+                moving = [
+                    jnp.broadcast_to(columns[slot_x, slot_y, slot_z, part, c : c + 1], (BLOCK, slots))
+                    for c in range(4)
+                ]
+                for z, own_row, damp, allow in zip(takers, fixed_rows, damps, allowed):
+                    dx = moving[0] - own_row[0]
+                    dy = moving[1] - own_row[1]
+                    dz = moving[2] - own_row[2]
+                    square = dx * dx + dy * dy + dz * dz + SOFTENING
+                    root = lax.rsqrt(square)
+                    root_two = root * root
+                    cube = root_two * root * allow
+                    arg = (square * square) * root * (damp * moving[3])
+                    fade = jnp.exp(arg)
+                    three = 1.0 - fade
+                    five = three + arg * fade
+                    direct = three * cube
+                    radial = five * cube * (3.0 * root_two)
+                    for number, value in ((0, radial), (2, direct)):
+                        high = value.astype(jnp.bfloat16)
+                        low = (value - high.astype(jnp.float32)).astype(jnp.bfloat16)
+                        links[line, nine, number, spot_at, part, z * slots : (z + 1) * slots] = high
+                        links[line, nine, number + 1, spot_at, part, z * slots : (z + 1) * slots] = low
+
+    def geometry_near(along_xs, zs):
+        def one(step, carry):
+            x = step % tiles[0]
+            y = step // tiles[0] % tiles[1]
+            to_y = step // (tiles[0] * tiles[1]) % tiles[1]
+            along_x = step // (tiles[0] * tiles[1] * tiles[1]) + along_xs[0]
+            geometry(x, y, along_x, to_y - y, zs)
+            return carry
+
+        lax.fori_loop(0, tiles[0] * tiles[1] * tiles[1] * len(along_xs), one, 0)
+
+    def geometry_far():
+        def one(step, carry):
+            x = step % tiles[0]
+            side = step // tiles[0] % 2
+            along_x = step // (2 * tiles[0]) - 1
+            geometry(x, side * (tiles[1] - 1), along_x, 2 * side - 1, levels)
+            return carry
+
+        lax.fori_loop(0, 6 * tiles[0], one, 0)
+
+    settle_all([x for x in every_x if 0 <= x < tiles[0]], near_y, own_z)
+    geometry_near([0], own_z)
+    off_diagonal = lax.broadcasted_iota(jnp.int32, (slots, slots), 0) != lax.broadcasted_iota(
+        jnp.int32, (slots, slots), 1
+    )
+    for x, y, z in places:
+        lanes = slice(z * slots, (z + 1) * slots)
+        for number in range(STREAMS):
+            link = links[x * tiles[1] + y, 4, number, levels.index(z), :, lanes].astype(jnp.float32)
+            links[x * tiles[1] + y, 4, number, levels.index(z), :, lanes] = jnp.where(
+                off_diagonal, link, 0.0
+            ).astype(jnp.bfloat16)
+
+    for move, copy in zip(moves, geom_copies):
+        if move[1][0] == 0:
+            copy.wait()
+    settle_all([x for x in every_x if 0 <= x < tiles[0]], near_y, side_z)
+    settle_all([-1], near_y, levels)
+    settle_all([tiles[0]], near_y, levels)
+    geometry_near([0], side_z)
+    geometry_near([-1], levels)
 
     everyone_wait(0, slots_a)
     total = jnp.sum(slots_a[...], axis=0)
@@ -306,127 +337,202 @@
         for h in range(1, past):
             value = value + coeffs[h] * past_sets[h + 1, t]
         held_one[x, y, z] = value
-    one_copies = halo(held_one, send_one, recv_one)
+    one_copies = halo(held_one, send_one, recv_one, rows)
     for copy in one_copies:
         copy.start()
+    geometry_near([1], levels)
     for move, copy in zip(moves, geom_copies):
-        if move[0][0] != 0:
+        if move[1][0] != 0:
             copy.wait()
-    settle_plane(jnp.int32(-1))
-    settle_plane(jnp.int32(tiles[0]))
-    lax.fori_loop(0, count * 6, other_x, 0)
-    off_diagonal = lax.broadcasted_iota(jnp.int32, (slots, slots), 0) != lax.broadcasted_iota(
-        jnp.int32, (slots, slots), 1
-    )
-    empty = jnp.zeros((slots, slots), jnp.bfloat16)
-    for t in range(count):
-        for number in range(STREAMS):
-            own_link = links[t, number, 13].astype(jnp.float32)
-            links[t, number, 13] = jnp.where(off_diagonal, own_link, 0.0).astype(jnp.bfloat16)
-            links[t, number, offsets] = empty
-    spread = wraps[0] * wraps[1] * wraps[2]
-    weights[spread] = empty
-
-    def weigh(held):
+    settle_all(every_x, far_y, levels)
+    geometry_far()
+
+    kinds = 5
+
+    def weigh(held, ys):
         def one(step, carry):
-            slot = (step // (wraps[1] * wraps[2]), step // wraps[2] % wraps[1], step % wraps[2])
-            moment = held[slot[0], slot[1], slot[2]]
-            along = moment * turns[0, slot[0], slot[1], slot[2]]
-            first = jnp.sum(jnp.where(row_of < 3, along, 0.0), axis=0, keepdims=True)
-            second = jnp.sum(jnp.where(row_of < 3, 0.0, along), axis=0, keepdims=True)
-            which = jnp.logical_or(row_of == 0, jnp.logical_and(row_of >= 2, row_of < 5))
-            both = jnp.where(which, first, second) * turns[1, slot[0], slot[1], slot[2]]
-            parts = [spots[slot[0], slot[1], slot[2], pl.ds(c, 1), :] * moment for c in range(3)]
-            value = jnp.concatenate(parts + [moment, both], axis=0)
-            high = value.astype(jnp.bfloat16).astype(jnp.float32)
-            rest = value - high
-            middle = rest.astype(jnp.bfloat16).astype(jnp.float32)
-            pad = jnp.zeros((slots - 3 * kinds * ROWS, slots), jnp.float32)
-            weights[step] = jnp.concatenate([high, middle, rest - middle, pad], axis=0).astype(jnp.bfloat16)
+            x = wrap(step - 1, wraps[0])
+            for y in ys:
+                for z in range(wraps[2]):
+                    slot = (x, y % wraps[1], z)
+                    moment = jnp.where(row_of < rows, held[slot], 0.0)
+                    along = moment * turns[(0,) + slot]
+                    first = jnp.sum(jnp.where(row_of < 3, along, 0.0), axis=0, keepdims=True)
+                    second = jnp.sum(jnp.where(row_of < 3, 0.0, along), axis=0, keepdims=True)
+                    which = jnp.logical_or(row_of == 0, jnp.logical_and(row_of >= 2, row_of < 5))
+                    both = jnp.where(which, first, second) * turns[(1,) + slot]
+                    tiles_of = [moment, both] + [
+                        spots[slot + (pl.ds(c, 1), slice(None))] * moment for c in range(3)
+                    ]
+                    parts = [[], [], []]
+                    for value in tiles_of:
+                        for level in range(3):
+                            piece = value.astype(jnp.bfloat16).astype(jnp.float32)
+                            parts[level].append(piece)
+                            value = value - piece
+                    order = [parts[0][0], parts[1][0], parts[2][0]]
+                    for level in range(3):
+                        order = order + parts[level][1:]
+                    order.append(jnp.zeros((ROWS, slots), jnp.float32))
+                    weights[slot] = jnp.concatenate(order, axis=0).astype(jnp.bfloat16)
             return carry
 
-        lax.fori_loop(0, spread, one, 0)
-
-    def field_of(t, sums):
-        x, y, z = spot(t)
-        radial = (sums[0:slots] + sums[slots : 2 * slots]).T
-        direct = (sums[2 * slots : 3 * slots] + sums[3 * slots : 4 * slots]).T
-
-        def tile(value, kind):
-            total = value[kind * ROWS : (kind + 1) * ROWS]
-            for level in (1, 2):
-                first = (level * kinds + kind) * ROWS
-                total = total + value[first : first + ROWS]
+        lax.fori_loop(0, wraps[0], one, 0)
+
+    def products(line, visits):
+        width = 2 * slots if len(levels) % 2 == 0 else slots
+        main = jnp.zeros((SPREAD, wide), jnp.float32)
+        rest = jnp.zeros((SPREAD_LOW, wide), jnp.float32)
+        plain = jnp.zeros((SPREAD_PLAIN, wide), jnp.float32)
+        per = width // slots
+        blank = jnp.zeros((slots, slots), jnp.bfloat16)
+        for nine, slot_x, slot_y in visits:
+            for start in range(0, len(levels), per):
+                chunk = range(start, start + per)
+                left = jnp.concatenate(
+                    [weights[slot_x, slot_y, levels[i] % wraps[2]] for i in chunk], axis=1
+                )
+
+                def matrix(number):
+                    lines = []
+                    for i in chunk:
+                        lines.append(
+                            jnp.concatenate(
+                                [
+                                    links[line, nine, number, i, :, z * slots : (z + 1) * slots]
+                                    if abs(levels[i] - z) <= 1
+                                    else blank
+                                    for z in range(tiles[2])
+                                ],
+                                axis=1,
+                            )
+                        )
+                    return jnp.concatenate(lines, axis=0)
+
+                def times(values, number):
+                    return jnp.dot(values, matrix(number), preferred_element_type=jnp.float32)
+
+                main = main + times(left, 0)
+                rest = rest + times(left[0:SPREAD_LOW], 1)
+                plain = plain + times(left[0:SPREAD_PLAIN], 2)
+                plain = plain + times(left[0:SPREAD_PLAIN], 3)
+        return main, rest, plain
+
+    def near_products(x, y):
+        visits = [
+            ((along + 1) * 3 + to_y - y + 1, wrap(x + along, wraps[0]), to_y)
+            for along in (-1, 0, 1)
+            for to_y in range(tiles[1])
+        ]
+        return products(x * tiles[1] + y, visits)
+
+    def far_products(x, y, side):
+        visits = [
+            ((along + 1) * 3 + 2 * side, wrap(x + along, wraps[0]), wrap((tiles[1] + 1) * side - 1, wraps[1]))
+            for along in (-1, 0, 1)
+        ]
+        return products(x * tiles[1] + y, visits)
+
+    def keep_near(step, carry):
+        x, y = step // tiles[1], step % tiles[1]
+        main, rest, plain = near_products(x, y)
+        partial_main[step] = main
+        partial_rest[step] = rest
+        partial_plain[step] = plain
+        return carry
+
+    def field_of(x, y, main, rest, plain):
+        def tile(value, index):
+            return value[index * ROWS : (index + 1) * ROWS]
+
+        def both_sum(first):
+            total = tile(main, first[0]) + tile(rest, first[0])
+            for index in first[1:]:
+                total = total + tile(main, index)
+                if (index + 1) * ROWS <= SPREAD_LOW:
+                    total = total + tile(rest, index)
             return total
 
-        turn = turns[0, x, y, z]
-        plain = tile(radial, 3)
-        both = tile(radial, 4)
-        inner = []
-        for c in range(3):
-            along = (tile(radial, c) - spots[x, y, z, pl.ds(c, 1), :] * plain) * turn
-            first = jnp.sum(jnp.where(row_of < 3, along, 0.0), axis=0, keepdims=True)
-            second = jnp.sum(jnp.where(row_of < 3, 0.0, along), axis=0, keepdims=True)
-            inner.append((first, second))
-        inner = jnp.concatenate(
-            [inner[c][0] for c in range(3)] + [inner[c][1] for c in range(3)] + [zero_row, zero_row], axis=0
-        )
-        lifted = jnp.concatenate([both[2:8], zero_row, zero_row], axis=0)
-        dots = jnp.where(row_of < 3, both[0:1], both[1:2])
-        return lifted - dots * turn - inner - tile(direct, 3)
-
-    def slot_at(base, k):
-        along = (k // 9 - 1, k // 3 % 3 - 1, k % 3 - 1)
-        slot = [wrap(base[i] + along[i], wraps[i]) for i in range(3)]
-        return (slot[0] * wraps[1] + slot[1]) * wraps[2] + slot[2]
-
-    def field(t):
-        base = spot(t)
-        sums = jnp.zeros((STREAMS * slots, slots), jnp.float32)
-        for pair in range(0, offsets, 2):
-            left = jnp.concatenate(
-                [
-                    jnp.concatenate([links[t, number, pair], links[t, number, pair + 1]], axis=1)
-                    for number in range(STREAMS)
-                ],
-                axis=0,
+        moment = both_sum((0, 1, 2))
+        both = both_sum((3, 7, 11))
+        lifts = [both_sum((4 + c, 8 + c, 12 + c)) for c in range(3)]
+        straight = tile(plain, 0) + tile(plain, 1) + tile(plain, 2)
+        result = []
+        for z in range(tiles[2]):
+            lanes = slice(z * slots, (z + 1) * slots)
+            turn = turns[0, x, y, z]
+            inner = []
+            for c in range(3):
+                along = (lifts[c][:, lanes] - spots[x, y, z, pl.ds(c, 1), :] * moment[:, lanes]) * turn
+                first = jnp.sum(jnp.where(row_of < 3, along, 0.0), axis=0, keepdims=True)
+                second = jnp.sum(jnp.where(row_of < 3, 0.0, along), axis=0, keepdims=True)
+                inner.append((first, second))
+            inner = jnp.concatenate(
+                [inner[c][0] for c in range(3)] + [inner[c][1] for c in range(3)] + [zero_row, zero_row], axis=0
             )
-            behind = spread if pair + 1 == offsets else slot_at(base, pair + 1)
-            right = jnp.concatenate([weights[slot_at(base, pair)], weights[behind]], axis=1)
-            sums = sums + lax.dot_general(
-                left, right, (((1,), (1,)), ((), ())), preferred_element_type=jnp.float32
-            )
-        return field_of(t, sums)
-
-    for copy in one_copies:
-        copy.wait()
-    weigh(held_one)
-
-    def first_pass(t, carry):
-        x, y, z = spot(t)
-        held_two[x, y, z] = (1.0 - RELAXATION) * held_one[x, y, z] + scaled[t] * (fixed[t] + field(t))
-        return carry
-
-    lax.fori_loop(0, count, first_pass, 0)
-    two_copies = halo(held_two, send_two, recv_two)
+            lifted = jnp.concatenate([both[2:8, lanes], zero_row, zero_row], axis=0)
+            dots = jnp.where(row_of < 3, both[0:1, lanes], both[1:2, lanes])
+            result.append(lifted - dots * turn - inner - straight[:, lanes])
+        return result
+
+    lines = tiles[0] * tiles[1]
+
+    def field(step, held, act):
+        x, y = step // tiles[1], step % tiles[1]
+        main, rest, plain = partial_main[step], partial_rest[step], partial_plain[step]
+        for side in range(2):
+            if tiles[1] == 1:
+                more = far_products(x, y, side)
+                main, rest, plain = main + more[0], rest + more[1], plain + more[2]
+        if tiles[1] > 1:
+            side = y // (tiles[1] - 1)
+            more = far_products(x, y, side)
+            keep = jnp.logical_or(y == 0, y == tiles[1] - 1).astype(jnp.float32)
+            if tiles[1] > 2:
+                more = tuple(jnp.where(keep > 0.5, value, 0.0) for value in more)
+            main, rest, plain = main + more[0], rest + more[1], plain + more[2]
+        fields = field_of(x, y, main, rest, plain)
+        for z in range(tiles[2]):
+            t = step * tiles[2] + z
+            act(x, y, z, t, (1.0 - RELAXATION) * held[x, y, z] + scaled[t] * (fixed[t] + fields[z]))
+
+    def sweep(held, copies, act):
+        for move, copy in zip(moves, copies):
+            if move[1][0] == 0:
+                copy.wait()
+        weigh(held, near_y)
+        lax.fori_loop(0, lines, keep_near, 0)
+        for move, copy in zip(moves, copies):
+            if move[1][0] != 0:
+                copy.wait()
+        weigh(held, far_y)
+
+        def one(step, carry):
+            field(step, held, act)
+            return carry
+
+        lax.fori_loop(0, lines, one, 0)
+
+    def first_act(x, y, z, t, value):
+        held_two[x, y, z] = value
+
+    sweep(held_one, one_copies, first_act)
+    two_copies = halo(held_two, send_two, recv_two, rows)
     for copy in two_copies:
         copy.start()
-    for copy in two_copies:
-        copy.wait()
-    weigh(held_two)
-
-    def second_pass(t, carry):
-        changed, size = carry
-        x, y, z = spot(t)
-        before = held_two[x, y, z]
-        after = (1.0 - RELAXATION) * before + scaled[t] * (fixed[t] + field(t))
+
+    def second_act(x, y, z, t, value):
+        held_one[x, y, z] = value
+
+    sweep(held_two, two_copies, second_act)
+    changed = jnp.zeros((ROWS, slots), jnp.float32)
+    size = jnp.zeros((ROWS, slots), jnp.float32)
+    for t, (x, y, z) in enumerate(places):
+        before, after = held_two[x, y, z], held_one[x, y, z]
         for c in range(rows):
             out_ref[c, x, y, z, :] = after[c]
         changed = changed + (after - before) * (after - before)
-        return changed, size + after * after
-
-    nothing = jnp.zeros((ROWS, slots), jnp.float32)
-    changed, size = lax.fori_loop(0, count, second_pass, (nothing, nothing))
+        size = size + after * after
 
     def all_of(value):
         return jnp.sum(jnp.sum(value, axis=0, keepdims=True), axis=1, keepdims=True)
@@ -449,6 +555,7 @@
         tiles = fractions.shape[1:4]
         slots = fractions.shape[4]
         count = tiles[0] * tiles[1] * tiles[2]
+        lines = tiles[0] * tiles[1]
         wraps = tuple(n + 2 for n in tiles)
         moves = len(halo_moves(devices, tiles))
         rows = history.shape[1]
@@ -473,11 +580,14 @@
                 pltpu.VMEM(wraps + (ROWS, slots), f32),
                 pltpu.VMEM(wraps + (ROWS, slots), f32),
                 pltpu.VMEM((history.shape[0], count, ROWS, slots), f32),
-                pltpu.VMEM((count, 4, slots, slots), f32),
                 pltpu.VMEM(wraps + (ROWS, slots), f32),
+                pltpu.VMEM(wraps + (slots, ROWS), f32),
                 pltpu.VMEM((2,) + wraps + (ROWS, slots), f32),
-                pltpu.VMEM((count, STREAMS, 28, slots, slots), jnp.bfloat16),
-                pltpu.VMEM((wraps[0] * wraps[1] * wraps[2] + 1, slots, slots), jnp.bfloat16),
+                pltpu.VMEM((lines, 9, STREAMS, wraps[2], slots, tiles[2] * slots), jnp.bfloat16),
+                pltpu.VMEM(wraps + (SPREAD, slots), jnp.bfloat16),
+                pltpu.VMEM((lines, SPREAD, tiles[2] * slots), f32),
+                pltpu.VMEM((lines, SPREAD_LOW, tiles[2] * slots), f32),
+                pltpu.VMEM((lines, SPREAD_PLAIN, tiles[2] * slots), f32),
                 pltpu.VMEM((count, ROWS, slots), f32),
                 pltpu.VMEM((count, ROWS, slots), f32),
                 pltpu.VMEM((total_devices, 1, slots), f32),

time: 48 us -> 40.4 us (0.84)
  Pallas kernels: 44.6 us -> 37.1 us
    pallas_call x1, Pallas kernels: 44.6 us -> 37.1 us  [on_device(): pl.pallas_call(functools.partial(kernel, devices), out_shape=(jax.ShapeDt...]
where the time goes in v2:
time: 40.4 us; the launch traced here: 40.2 us
  Pallas kernels  37.1 us (92%)
  between operations  1.81 us (4%)
  local copies, waits for them, and re-layouts  1.31 us (3%)
    pallas_call x1, Pallas kernels, on_device(): pl.pallas_call(functools.partial(kernel, devices), out_shape=(jax.ShapeDt...  37.1 us
    unnamed x3, local copies, waits for them, and re-layouts  1.31 us

profile of v2, /device:TPU:0, one launch (start us, length us, event | category | flops | bytes accessed | tf_op | source)
XLA Modules:
  0.0 40.2 jit_solution(2786597627200357186)
XLA Ops:
  0.6 37.1 %shard_map.77 = (f32[6,1,2,2,128]{4,3,2,1,0:T(2,128)}, f32[1,128]{1,0:T(1,128)}) custom-call(f32[3,1,2,2,128]{4,3,2,1,0:T(2,128)} %frac_in.1, f32[1,2,2,128]{3,2,1,0:T(2,128)} %pol_in.1, s32[1,2,2,128]{3,2,1,0:T(2,128)} %occ_in.1, s32[1,2,2,27]{3,2,1,0:T(2,128)} %mask_in.1, f32[6,1,2,2,128]{4,3,2,1,0:T(2,128)} %perm_in.1, f32[6,6,1,2,2,128]{5,4,3,2,1,0:T(2,128)} %hist_in.1), custom_call_target="tpu_custom_call" | custom-call | tf_op jit(solution)/shard_map/pallas_call | solution.py:564
  37.7 0.0 copy-start
  37.7 1.3 %copy.10 = f32[6,1,2,2,128]{4,3,2,1,0:T(2,128)} copy(f32[6,1,2,2,128]{4,3,2,1,0:T(2,128)} %get-tuple-element.8) | data formatting | bytes 24576
  39.0 0.0 copy-done
Async XLA Ops:
  37.7 1.3 %copy-start = (f32[1,128]{1,0:T(1,128)S(1)}, f32[1,128]{1,0:T(1,128)}, u32[]{:S(2)}) copy-start(f32[1,128]{1,0:T(1,128)} %get-tuple-element.5) | copy-start | bytes 1540

commit v3 on v2

--- a/solution.py
+++ b/solution.py
@@ -14,7 +14,8 @@
 MESH = pl.DeviceIdType.MESH
 AXES = ("gx", "gy", "gz")
 ROWS = 8
-BLOCK = 32
+BLOCK = 16
+APART = 2.5e25
 STREAMS = 4
 SPREAD = 128
 SPREAD_LOW = 96
@@ -73,7 +74,8 @@
 def kernel(
     devices,
     frac_in, pol_in, occ_in, mask_in, perm_in, hist_in,
-    out_ref, change_ref,
+    out_hbm, change_ref,
+    out_ref,
     frac_ref, pol_ref, occ_ref, mask_ref, perm_ref, hist_ref,
     geom, held_one, held_two, past_sets, spots, columns, turns, links, weights,
     partial_main, partial_rest, partial_plain, scaled, fixed, slots_a, slots_b,
@@ -258,7 +260,10 @@
             slot_z = level % wraps[2]
             takers = [z for z in range(tiles[2]) if abs(level - z) <= 1]
             fixed_rows = [[spots[x, y, z, pl.ds(c, 1), :] for c in range(4)] for z in takers]
-            allowed = [mask_ref[x, y, z, nine * 3 + level - z + 1].astype(jnp.float32) for z in takers]
+            softs = [
+                SOFTENING + (1 - mask_ref[x, y, z, nine * 3 + level - z + 1]).astype(jnp.float32) * APART
+                for z in takers
+            ]
             damps = [own_row[3] * -THOLE_DAMP for own_row in fixed_rows]
             for first in range(0, slots, BLOCK):
                 part = pl.ds(first, BLOCK)
@@ -266,20 +271,18 @@
                     jnp.broadcast_to(columns[slot_x, slot_y, slot_z, part, c : c + 1], (BLOCK, slots))
                     for c in range(4)
                 ]
-                for z, own_row, damp, allow in zip(takers, fixed_rows, damps, allowed):
+                for z, own_row, damp, soft in zip(takers, fixed_rows, damps, softs):
                     dx = moving[0] - own_row[0]
                     dy = moving[1] - own_row[1]
                     dz = moving[2] - own_row[2]
-                    square = dx * dx + dy * dy + dz * dz + SOFTENING
+                    square = dx * dx + dy * dy + dz * dz + soft
                     root = lax.rsqrt(square)
                     root_two = root * root
-                    cube = root_two * root * allow
-                    arg = (square * square) * root * (damp * moving[3])
-                    fade = jnp.exp(arg)
-                    three = 1.0 - fade
-                    five = three + arg * fade
-                    direct = three * cube
-                    radial = five * cube * (3.0 * root_two)
+                    cube = root_two * root
+                    arg = (square * root) * square * (damp * moving[3])
+                    faded = jnp.exp(arg) * cube
+                    direct = cube - faded
+                    radial = (direct + arg * faded) * root_two
                     for number, value in ((0, radial), (2, direct)):
                         high = value.astype(jnp.bfloat16)
                         low = (value - high.astype(jnp.float32)).astype(jnp.bfloat16)
@@ -472,7 +475,7 @@
             )
             lifted = jnp.concatenate([both[2:8, lanes], zero_row, zero_row], axis=0)
             dots = jnp.where(row_of < 3, both[0:1, lanes], both[1:2, lanes])
-            result.append(lifted - dots * turn - inner - straight[:, lanes])
+            result.append(3.0 * (lifted - dots * turn - inner) - straight[:, lanes])
         return result
 
     lines = tiles[0] * tiles[1]
@@ -501,7 +504,7 @@
             if move[1][0] == 0:
                 copy.wait()
         weigh(held, near_y)
-        lax.fori_loop(0, lines, keep_near, 0)
+        lax.fori_loop(0, lines, keep_near, 0, unroll=True)
         for move, copy in zip(moves, copies):
             if move[1][0] != 0:
                 copy.wait()
@@ -511,7 +514,7 @@
             field(step, held, act)
             return carry
 
-        lax.fori_loop(0, lines, one, 0)
+        lax.fori_loop(0, lines, one, 0, unroll=True)
 
     def first_act(x, y, z, t, value):
         held_two[x, y, z] = value
@@ -533,6 +536,8 @@
             out_ref[c, x, y, z, :] = after[c]
         changed = changed + (after - before) * (after - before)
         size = size + after * after
+    put = pltpu.make_async_copy(out_ref, out_hbm, load_sem.at[len(loads)])
+    put.start()
 
     def all_of(value):
         return jnp.sum(jnp.sum(value, axis=0, keepdims=True), axis=1, keepdims=True)
@@ -545,6 +550,7 @@
     above = jnp.sum(jnp.where(lane == 0, pair, 0.0), axis=1, keepdims=True)
     below = jnp.sum(jnp.where(lane == 1, pair, 0.0), axis=1, keepdims=True)
     change_ref[...] = jnp.broadcast_to(jnp.sqrt(above / (below + 1.0)), (1, slots))
+    put.wait()
 
 
 def solution(mesh):
@@ -568,8 +574,9 @@
                 jax.ShapeDtypeStruct((1, slots), f32),
             ),
             in_specs=[pl.BlockSpec(memory_space=pltpu.HBM)] * 6,
-            out_specs=(vmem, vmem),
+            out_specs=(pl.BlockSpec(memory_space=pltpu.HBM), vmem),
             scratch_shapes=[
+                pltpu.VMEM(perm_field.shape, f32),
                 pltpu.VMEM(fractions.shape, f32),
                 pltpu.VMEM(polarizability.shape, f32),
                 pltpu.VMEM(occupancy.shape, jnp.int32),
@@ -592,7 +599,7 @@
                 pltpu.VMEM((count, ROWS, slots), f32),
                 pltpu.VMEM((total_devices, 1, slots), f32),
                 pltpu.VMEM((total_devices, 1, slots), f32),
-                pltpu.SemaphoreType.DMA((6,)),
+                pltpu.SemaphoreType.DMA((7,)),
                 pltpu.SemaphoreType.DMA((2,)),
                 pltpu.SemaphoreType.DMA((2,)),
             ]

time: 40.4 us -> 39.7 us (0.983)
  Pallas kernels: 37.1 us -> 36.4 us
    pallas_call x1, Pallas kernels: 37.1 us -> 36.4 us  [on_device(): pl.pallas_call(functools.partial(kernel, devices), out_shape=(jax.ShapeDt...]
where the time goes in v3:
time: 39.7 us; the launch traced here: 39.5 us
  Pallas kernels  36.4 us (92%)
  between operations  1.81 us (5%)
  local copies, waits for them, and re-layouts  1.31 us (3%)
    pallas_call x1, Pallas kernels, on_device(): pl.pallas_call(functools.partial(kernel, devices), out_shape=(jax.ShapeDt...  36.4 us
    unnamed x3, local copies, waits for them, and re-layouts  1.31 us

profile of v3, /device:TPU:0, one launch (start us, length us, event | category | flops | bytes accessed | tf_op | source)
XLA Modules:
  0.0 39.5 jit_solution(13354379318441764012)
XLA Ops:
  0.6 36.4 %shard_map.77 = (f32[6,1,2,2,128]{4,3,2,1,0:T(2,128)}, f32[1,128]{1,0:T(1,128)}) custom-call(f32[3,1,2,2,128]{4,3,2,1,0:T(2,128)} %frac_in.1, f32[1,2,2,128]{3,2,1,0:T(2,128)} %pol_in.1, s32[1,2,2,128]{3,2,1,0:T(2,128)} %occ_in.1, s32[1,2,2,27]{3,2,1,0:T(2,128)} %mask_in.1, f32[6,1,2,2,128]{4,3,2,1,0:T(2,128)} %perm_in.1, f32[6,6,1,2,2,128]{5,4,3,2,1,0:T(2,128)} %hist_in.1), custom_call_target="tpu_custom_call" | custom-call | tf_op jit(solution)/shard_map/pallas_call | solution.py:570
  37.0 0.0 copy-start
  37.0 1.3 %copy.10 = f32[6,1,2,2,128]{4,3,2,1,0:T(2,128)} copy(f32[6,1,2,2,128]{4,3,2,1,0:T(2,128)} %get-tuple-element.8) | data formatting | bytes 24576
  38.3 0.0 copy-done
Async XLA Ops:
  37.0 1.3 %copy-start = (f32[1,128]{1,0:T(1,128)S(1)}, f32[1,128]{1,0:T(1,128)}, u32[]{:S(2)}) copy-start(f32[1,128]{1,0:T(1,128)} %get-tuple-element.5) | copy-start | bytes 1540

commit v4 on v3

--- a/solution.py
+++ b/solution.py
@@ -77,7 +77,7 @@
     out_hbm, change_ref,
     out_ref,
     frac_ref, pol_ref, occ_ref, mask_ref, perm_ref, hist_ref,
-    geom, held_one, held_two, past_sets, spots, columns, turns, links, weights,
+    geom, held_one, held_two, past_sets, spots, features, distance, damping, turns, links, weights,
     partial_main, partial_rest, partial_plain, scaled, fixed, slots_a, slots_b,
     load_sem, send_all, recv_all, send_geom, recv_geom, send_one, recv_one, send_two, recv_two,
 ):
@@ -89,7 +89,7 @@
     total_devices = devices[0] * devices[1] * devices[2]
     at = [lax.axis_index(axis) for axis in AXES]
     me = (at[0] * devices[1] + at[1]) * devices[2] + at[2]
-    moves = halo_moves(devices, tiles)
+    moves = sorted(halo_moves(devices, tiles), key=lambda move: (move[1][0] != 0, sum(abs(part[0]) for part in move)))
     lane = lax.broadcasted_iota(jnp.int32, (1, slots), 1)
     loads = [
         pltpu.make_async_copy(source, target, load_sem.at[number])
@@ -105,20 +105,19 @@
 
     def each_other(act):
         def pair(step, carry):
-            ahead = (step // devices[1], step % devices[1])
-            first = []
-            for axis in range(2):
-                place = at[axis] + ahead[axis]
-                first.append(jnp.where(place >= devices[axis], place - devices[axis], place))
+            down, across = step // devices[0], step % devices[0]
+            x = at[0] + across
+            x = jnp.where(x >= devices[0], x - devices[0], x)
+            y = jnp.where(2 * at[1] < devices[1], devices[1] - 1 - down, down)
             for shift in range(devices[2] - 1, -1, -1):
                 last = at[2] + shift
                 last = jnp.where(last >= devices[2], last - devices[2], last)
                 if shift == 0:
-                    @pl.when(step > 0)
+                    @pl.when(jnp.logical_or(across > 0, y != at[1]))
                     def _():
-                        act((first[0], first[1], last))
+                        act((x, y, last))
                 else:
-                    act((first[0], first[1], last))
+                    act((x, y, last))
             return carry
 
         lax.fori_loop(0, devices[0] * devices[1], pair, 0)
@@ -222,6 +221,58 @@
     def wrap(value, size):
         return jnp.where(value < 0, value + size, value)
 
+    def pieces(value):
+        high = value.astype(jnp.bfloat16).astype(jnp.float32)
+        value = value - high
+        middle = value.astype(jnp.bfloat16).astype(jnp.float32)
+        return high, middle, value - middle
+
+    def choose(values):
+        result = values[0]
+        for row, value in enumerate(values[1:], 1):
+            result = jnp.where(row_of == row, value, result)
+        return result
+
+    one_tile = jnp.ones((ROWS, slots), jnp.float32)
+    zero_tile = jnp.zeros((ROWS, slots), jnp.float32)
+
+    def broad(slot, c):
+        return jnp.broadcast_to(spots[slot[0], slot[1], slot[2], pl.ds(c, 1), :], (ROWS, slots))
+
+    def padded(parts):
+        return parts + [zero_tile] * (slots // ROWS - len(parts))
+
+    def source_features(slot):
+        parts = []
+        for c in range(3):
+            value = broad(slot, c)
+            high, middle, low = pieces(value)
+            square, square_middle, square_low = pieces(value * value)
+            parts.append(
+                choose([square, one_tile, high, square_middle, high, middle, one_tile, square_low])
+            )
+            parts.append(choose([middle, high, low, one_tile, middle, low, zero_tile, zero_tile]))
+        high, middle, low = pieces(broad(slot, 3))
+        parts.append(choose([high, high, middle, high, low, middle, middle, low]))
+        return jnp.concatenate(padded(parts), axis=0).astype(jnp.bfloat16)
+
+    def taker_features(slot):
+        parts = []
+        for c in range(3):
+            value = broad(slot, c)
+            high, middle, low = pieces(value)
+            square, square_middle, square_low = pieces(value * value)
+            high, middle, low = -2.0 * high, -2.0 * middle, -2.0 * low
+            parts.append(
+                choose([one_tile, square, high, one_tile, middle, high, square_middle, one_tile])
+            )
+            parts.append(choose([middle, low, high, square_low, low, middle, zero_tile, zero_tile]))
+        high, middle, low = pieces(broad(slot, 3) * -THOLE_DAMP)
+        damp = choose([high, middle, high, low, high, middle, low, middle])
+        far = jnp.concatenate(padded(parts), axis=0).astype(jnp.bfloat16)
+        fade = jnp.concatenate(padded([zero_tile] * len(parts) + [damp]), axis=0).astype(jnp.bfloat16)
+        return far, fade
+
     def settle(place, slot):
         tile = geom[slot[0], slot[1], slot[2]]
         shift = jnp.zeros((ROWS, slots), jnp.float32)
@@ -230,7 +281,7 @@
             shift = jnp.where(row_of == axis, corner, shift)
         tile = tile + shift
         spots[slot[0], slot[1], slot[2]] = tile
-        columns[slot[0], slot[1], slot[2]] = tile.T
+        features[slot[0], slot[1], slot[2]] = source_features(slot).T
         one = jnp.ones((2, slots), jnp.float32)
         turns[0, slot[0], slot[1], slot[2]] = jnp.concatenate(
             [tile[0:3], tile[0:3], jnp.zeros((2, slots), jnp.float32)], axis=0
@@ -259,27 +310,24 @@
             spot_at = levels.index(level)
             slot_z = level % wraps[2]
             takers = [z for z in range(tiles[2]) if abs(level - z) <= 1]
-            fixed_rows = [[spots[x, y, z, pl.ds(c, 1), :] for c in range(4)] for z in takers]
             softs = [
                 SOFTENING + (1 - mask_ref[x, y, z, nine * 3 + level - z + 1]).astype(jnp.float32) * APART
                 for z in takers
             ]
-            damps = [own_row[3] * -THOLE_DAMP for own_row in fixed_rows]
+            lanes = slice(takers[0] * slots, (takers[-1] + 1) * slots)
+            left = features[slot_x, slot_y, slot_z]
+            squares = jnp.dot(left, distance[line, :, lanes], preferred_element_type=jnp.float32)
+            damps = jnp.dot(left, damping[line, :, lanes], preferred_element_type=jnp.float32)
             for first in range(0, slots, BLOCK):
                 part = pl.ds(first, BLOCK)
-                moving = [
-                    jnp.broadcast_to(columns[slot_x, slot_y, slot_z, part, c : c + 1], (BLOCK, slots))
-                    for c in range(4)
-                ]
-                for z, own_row, damp, soft in zip(takers, fixed_rows, damps, softs):
-                    dx = moving[0] - own_row[0]
-                    dy = moving[1] - own_row[1]
-                    dz = moving[2] - own_row[2]
-                    square = dx * dx + dy * dy + dz * dz + soft
+                for z, soft in zip(takers, softs):
+                    at_lane = (z - takers[0]) * slots
+                    square = squares[first : first + BLOCK, at_lane : at_lane + slots] + soft
+                    damp = damps[first : first + BLOCK, at_lane : at_lane + slots]
                     root = lax.rsqrt(square)
                     root_two = root * root
                     cube = root_two * root
-                    arg = (square * root) * square * (damp * moving[3])
+                    arg = (square * root) * square * damp
                     faded = jnp.exp(arg) * cube
                     direct = cube - faded
                     radial = (direct + arg * faded) * root_two
@@ -289,16 +337,24 @@
                         links[line, nine, number, spot_at, part, z * slots : (z + 1) * slots] = high
                         links[line, nine, number + 1, spot_at, part, z * slots : (z + 1) * slots] = low
 
-    def geometry_near(along_xs, zs):
+    def geometry_near(along_x, zs):
         def one(step, carry):
             x = step % tiles[0]
             y = step // tiles[0] % tiles[1]
-            to_y = step // (tiles[0] * tiles[1]) % tiles[1]
-            along_x = step // (tiles[0] * tiles[1] * tiles[1]) + along_xs[0]
+            to_y = step // (tiles[0] * tiles[1])
             geometry(x, y, along_x, to_y - y, zs)
             return carry
 
-        lax.fori_loop(0, tiles[0] * tiles[1] * tiles[1] * len(along_xs), one, 0)
+        lax.fori_loop(0, tiles[0] * tiles[1] * tiles[1], one, 0, unroll=True)
+
+    def arrive(copies, kinds_of):
+        for move, copy in zip(moves, copies):
+            if move[1][0] != 0:
+                kind = "far"
+            else:
+                kind = ("x" if move[0][0] != 0 else "") + ("z" if move[2][0] != 0 else "")
+            if kind in kinds_of:
+                copy.wait()
 
     def geometry_far():
         def one(step, carry):
@@ -308,10 +364,16 @@
             geometry(x, side * (tiles[1] - 1), along_x, 2 * side - 1, levels)
             return carry
 
-        lax.fori_loop(0, 6 * tiles[0], one, 0)
-
-    settle_all([x for x in every_x if 0 <= x < tiles[0]], near_y, own_z)
-    geometry_near([0], own_z)
+        lax.fori_loop(0, 6 * tiles[0], one, 0, unroll=True)
+
+    own_x = list(range(tiles[0]))
+    settle_all(own_x, near_y, own_z)
+    for x, y, z in places:
+        lanes = slice(z * slots, (z + 1) * slots)
+        far, fade = taker_features((x, y, z))
+        distance[x * tiles[1] + y, :, lanes] = far
+        damping[x * tiles[1] + y, :, lanes] = fade
+    geometry_near(0, own_z)
     off_diagonal = lax.broadcasted_iota(jnp.int32, (slots, slots), 0) != lax.broadcasted_iota(
         jnp.int32, (slots, slots), 1
     )
@@ -323,14 +385,13 @@
                 off_diagonal, link, 0.0
             ).astype(jnp.bfloat16)
 
-    for move, copy in zip(moves, geom_copies):
-        if move[1][0] == 0:
-            copy.wait()
-    settle_all([x for x in every_x if 0 <= x < tiles[0]], near_y, side_z)
+    arrive(geom_copies, ("z",))
+    settle_all(own_x, near_y, side_z)
+    geometry_near(0, side_z)
+    arrive(geom_copies, ("x", "xz"))
     settle_all([-1], near_y, levels)
     settle_all([tiles[0]], near_y, levels)
-    geometry_near([0], side_z)
-    geometry_near([-1], levels)
+    geometry_near(-1, levels)
 
     everyone_wait(0, slots_a)
     total = jnp.sum(slots_a[...], axis=0)
@@ -343,21 +404,19 @@
     one_copies = halo(held_one, send_one, recv_one, rows)
     for copy in one_copies:
         copy.start()
-    geometry_near([1], levels)
-    for move, copy in zip(moves, geom_copies):
-        if move[1][0] != 0:
-            copy.wait()
+    geometry_near(1, levels)
+    arrive(geom_copies, ("far",))
     settle_all(every_x, far_y, levels)
-    geometry_far()
 
     kinds = 5
 
-    def weigh(held, ys):
+    def weigh(held, xs, ys, zs):
         def one(step, carry):
-            x = wrap(step - 1, wraps[0])
+            x = step * (xs[1] - xs[0] if len(xs) > 1 else 1) + xs[0]
+            x = wrap(x, wraps[0])
             for y in ys:
-                for z in range(wraps[2]):
-                    slot = (x, y % wraps[1], z)
+                for z in zs:
+                    slot = (x, y % wraps[1], z % wraps[2])
                     moment = jnp.where(row_of < rows, held[slot], 0.0)
                     along = moment * turns[(0,) + slot]
                     first = jnp.sum(jnp.where(row_of < 3, along, 0.0), axis=0, keepdims=True)
@@ -380,18 +439,16 @@
                     weights[slot] = jnp.concatenate(order, axis=0).astype(jnp.bfloat16)
             return carry
 
-        lax.fori_loop(0, wraps[0], one, 0)
+        lax.fori_loop(0, len(xs), one, 0)
 
     def products(line, visits):
-        width = 2 * slots if len(levels) % 2 == 0 else slots
         main = jnp.zeros((SPREAD, wide), jnp.float32)
         rest = jnp.zeros((SPREAD_LOW, wide), jnp.float32)
         plain = jnp.zeros((SPREAD_PLAIN, wide), jnp.float32)
-        per = width // slots
         blank = jnp.zeros((slots, slots), jnp.bfloat16)
-        for nine, slot_x, slot_y in visits:
-            for start in range(0, len(levels), per):
-                chunk = range(start, start + per)
+        for nine, slot_x, slot_y, zs in visits:
+            for start in range(0, len(zs), 2):
+                chunk = [levels.index(z) for z in zs[start : start + 2]]
                 left = jnp.concatenate(
                     [weights[slot_x, slot_y, levels[i] % wraps[2]] for i in chunk], axis=1
                 )
@@ -421,28 +478,31 @@
                 plain = plain + times(left[0:SPREAD_PLAIN], 3)
         return main, rest, plain
 
-    def near_products(x, y):
+    def near_products(x, y, parts):
         visits = [
-            ((along + 1) * 3 + to_y - y + 1, wrap(x + along, wraps[0]), to_y)
-            for along in (-1, 0, 1)
+            ((along + 1) * 3 + to_y - y + 1, wrap(x + along, wraps[0]), to_y, zs)
+            for along, zs in parts
             for to_y in range(tiles[1])
         ]
         return products(x * tiles[1] + y, visits)
 
     def far_products(x, y, side):
         visits = [
-            ((along + 1) * 3 + 2 * side, wrap(x + along, wraps[0]), wrap((tiles[1] + 1) * side - 1, wraps[1]))
+            ((along + 1) * 3 + 2 * side, wrap(x + along, wraps[0]), wrap((tiles[1] + 1) * side - 1, wraps[1]), levels)
             for along in (-1, 0, 1)
         ]
         return products(x * tiles[1] + y, visits)
 
-    def keep_near(step, carry):
-        x, y = step // tiles[1], step % tiles[1]
-        main, rest, plain = near_products(x, y)
-        partial_main[step] = main
-        partial_rest[step] = rest
-        partial_plain[step] = plain
-        return carry
+    partials = (partial_main, partial_rest, partial_plain)
+
+    def gather(parts, start):
+        def one(step, carry):
+            sums = near_products(step // tiles[1], step % tiles[1], parts)
+            for partial, value in zip(partials, sums):
+                partial[step] = value if start else partial[step] + value
+            return carry
+
+        lax.fori_loop(0, tiles[0] * tiles[1], one, 0, unroll=True)
 
     def field_of(x, y, main, rest, plain):
         def tile(value, index):
@@ -499,16 +559,31 @@
             t = step * tiles[2] + z
             act(x, y, z, t, (1.0 - RELAXATION) * held[x, y, z] + scaled[t] * (fixed[t] + fields[z]))
 
+    edge_x = [-1, tiles[0]]
+
+    def first_near(held, copies):
+        weigh(held, own_x, near_y, own_z)
+        gather([(0, own_z)], True)
+        geometry_far()
+        arrive(copies, ("x", "z", "xz"))
+        weigh(held, own_x, near_y, side_z)
+        weigh(held, edge_x, near_y, levels)
+        gather([(0, side_z), (-1, levels), (1, levels)], False)
+
+    def second_near(held, copies):
+        weigh(held, own_x, near_y, own_z)
+        gather([(0, own_z)], True)
+        arrive(copies, ("x", "z"))
+        weigh(held, own_x, near_y, side_z)
+        weigh(held, edge_x, near_y, own_z)
+        gather([(0, side_z), (-1, own_z), (1, own_z)], False)
+        arrive(copies, ("xz",))
+        weigh(held, edge_x, near_y, side_z)
+        gather([(-1, side_z), (1, side_z)], False)
+
     def sweep(held, copies, act):
-        for move, copy in zip(moves, copies):
-            if move[1][0] == 0:
-                copy.wait()
-        weigh(held, near_y)
-        lax.fori_loop(0, lines, keep_near, 0, unroll=True)
-        for move, copy in zip(moves, copies):
-            if move[1][0] != 0:
-                copy.wait()
-        weigh(held, far_y)
+        arrive(copies, ("far",))
+        weigh(held, every_x, far_y, levels)
 
         def one(step, carry):
             field(step, held, act)
@@ -519,6 +594,7 @@
     def first_act(x, y, z, t, value):
         held_two[x, y, z] = value
 
+    first_near(held_one, one_copies)
     sweep(held_one, one_copies, first_act)
     two_copies = halo(held_two, send_two, recv_two, rows)
     for copy in two_copies:
@@ -527,6 +603,7 @@
     def second_act(x, y, z, t, value):
         held_one[x, y, z] = value
 
+    second_near(held_two, two_copies)
     sweep(held_two, two_copies, second_act)
     changed = jnp.zeros((ROWS, slots), jnp.float32)
     size = jnp.zeros((ROWS, slots), jnp.float32)
@@ -539,16 +616,15 @@
     put = pltpu.make_async_copy(out_ref, out_hbm, load_sem.at[len(loads)])
     put.start()
 
-    def all_of(value):
-        return jnp.sum(jnp.sum(value, axis=0, keepdims=True), axis=1, keepdims=True)
-
-    pair = jnp.where(lane == 0, all_of(changed), jnp.where(lane == 1, all_of(size), 0.0))
-    slots_b[pl.ds(me, 1)] = pair.reshape(1, 1, slots)
+    pair = jnp.concatenate(
+        [jnp.sum(value, axis=0, keepdims=True) for value in (changed, size)], axis=1
+    )
+    slots_b[pl.ds(me, 1)] = pair.reshape(1, 1, 2 * slots)
     everyone(1, slots_b)
     everyone_wait(1, slots_b)
     pair = jnp.sum(slots_b[...], axis=0)
-    above = jnp.sum(jnp.where(lane == 0, pair, 0.0), axis=1, keepdims=True)
-    below = jnp.sum(jnp.where(lane == 1, pair, 0.0), axis=1, keepdims=True)
+    above = jnp.sum(pair[:, 0:slots], axis=1, keepdims=True)
+    below = jnp.sum(pair[:, slots : 2 * slots], axis=1, keepdims=True)
     change_ref[...] = jnp.broadcast_to(jnp.sqrt(above / (below + 1.0)), (1, slots))
     put.wait()
 
@@ -588,7 +664,9 @@
                 pltpu.VMEM(wraps + (ROWS, slots), f32),
                 pltpu.VMEM((history.shape[0], count, ROWS, slots), f32),
                 pltpu.VMEM(wraps + (ROWS, slots), f32),
-                pltpu.VMEM(wraps + (slots, ROWS), f32),
+                pltpu.VMEM(wraps + (slots, slots), jnp.bfloat16),
+                pltpu.VMEM((lines, slots, tiles[2] * slots), jnp.bfloat16),
+                pltpu.VMEM((lines, slots, tiles[2] * slots), jnp.bfloat16),
                 pltpu.VMEM((2,) + wraps + (ROWS, slots), f32),
                 pltpu.VMEM((lines, 9, STREAMS, wraps[2], slots, tiles[2] * slots), jnp.bfloat16),
                 pltpu.VMEM(wraps + (SPREAD, slots), jnp.bfloat16),
@@ -598,7 +676,7 @@
                 pltpu.VMEM((count, ROWS, slots), f32),
                 pltpu.VMEM((count, ROWS, slots), f32),
                 pltpu.VMEM((total_devices, 1, slots), f32),
-                pltpu.VMEM((total_devices, 1, slots), f32),
+                pltpu.VMEM((total_devices, 1, 2 * slots), f32),
                 pltpu.SemaphoreType.DMA((7,)),
                 pltpu.SemaphoreType.DMA((2,)),
                 pltpu.SemaphoreType.DMA((2,)),

time: 39.7 us -> 35.4 us (0.89)
  Pallas kernels: 36.4 us -> 32 us
    pallas_call x1, Pallas kernels: 36.4 us -> 32 us  [on_device(): pl.pallas_call(functools.partial(kernel, devices), out_shape=(jax.ShapeDt...]
where the time goes in v4:
time: 35.4 us; the launch traced here: 35.1 us
  Pallas kernels  32 us (90%)
  between operations  1.81 us (5%)
  local copies, waits for them, and re-layouts  1.31 us (4%)
    pallas_call x1, Pallas kernels, on_device(): pl.pallas_call(functools.partial(kernel, devices), out_shape=(jax.ShapeDt...  32 us
    unnamed x3, local copies, waits for them, and re-layouts  1.31 us

profile of v4, /device:TPU:0, one launch (start us, length us, event | category | flops | bytes accessed | tf_op | source)
XLA Modules:
  0.0 35.1 jit_solution(2482618547321837982)
XLA Ops:
  0.6 32.0 %shard_map.77 = (f32[6,1,2,2,128]{4,3,2,1,0:T(2,128)}, f32[1,128]{1,0:T(1,128)}) custom-call(f32[3,1,2,2,128]{4,3,2,1,0:T(2,128)} %frac_in.1, f32[1,2,2,128]{3,2,1,0:T(2,128)} %pol_in.1, s32[1,2,2,128]{3,2,1,0:T(2,128)} %occ_in.1, s32[1,2,2,27]{3,2,1,0:T(2,128)} %mask_in.1, f32[6,1,2,2,128]{4,3,2,1,0:T(2,128)} %perm_in.1, f32[6,6,1,2,2,128]{5,4,3,2,1,0:T(2,128)} %hist_in.1), custom_call_target="tpu_custom_call" | custom-call | tf_op jit(solution)/shard_map/pallas_call | solution.py:646
  32.7 0.0 copy-start
  32.7 1.3 %copy.10 = f32[6,1,2,2,128]{4,3,2,1,0:T(2,128)} copy(f32[6,1,2,2,128]{4,3,2,1,0:T(2,128)} %get-tuple-element.8) | data formatting | bytes 24576
  34.0 0.0 copy-done
Async XLA Ops:
  32.7 1.3 %copy-start = (f32[1,128]{1,0:T(1,128)S(1)}, f32[1,128]{1,0:T(1,128)}, u32[]{:S(2)}) copy-start(f32[1,128]{1,0:T(1,128)} %get-tuple-element.5) | copy-start | bytes 1540

commit v5 on v4

--- a/solution.py
+++ b/solution.py
@@ -77,7 +77,7 @@
     out_hbm, change_ref,
     out_ref,
     frac_ref, pol_ref, occ_ref, mask_ref, perm_ref, hist_ref,
-    geom, held_one, held_two, past_sets, spots, features, distance, damping, turns, links, weights,
+    geom, held_one, held_two, past_sets, spots, split_ref, features, distance, damping, turns, links, weights,
     partial_main, partial_rest, partial_plain, scaled, fixed, slots_a, slots_b,
     load_sem, send_all, recv_all, send_geom, recv_geom, send_one, recv_one, send_two, recv_two,
 ):
@@ -120,7 +120,7 @@
                     act((x, y, last))
             return carry
 
-        lax.fori_loop(0, devices[0] * devices[1], pair, 0)
+        lax.fori_loop(0, devices[0] * devices[1], pair, 0, unroll=4)
 
     barrier = pltpu.get_barrier_semaphore()
 
@@ -172,6 +172,33 @@
                 )
             )
         return copies
+
+    x_moves = {
+        move[0][0]: number
+        for number, move in enumerate(moves)
+        if move[0][0] != 0 and move[1][0] == 0 and move[2][0] == 0
+    }
+    if len(x_moves) == 2:
+        first_x = jnp.where(at[0] % 2 == 0, 1, -1)
+        second_x = -first_x
+        first_move = jnp.where(at[0] % 2 == 0, x_moves[-1], x_moves[1])
+        second_move = x_moves[-1] + x_moves[1] - first_move
+    else:
+        first_x, second_x = 1, -1
+        first_move, second_move = x_moves[1], None
+
+    def arrive_x(held, send, recv, depth, number):
+        if number is None:
+            return
+        move = moves[x_moves[1]]
+        pltpu.make_async_remote_copy(
+            src_ref=held.at[tuple(pl.ds(part[1], part[2]) for part in move) + (pl.ds(0, depth),)],
+            dst_ref=held.at[tuple(pl.ds(part[3], part[2]) for part in move) + (pl.ds(0, depth),)],
+            send_sem=send.at[number],
+            recv_sem=recv.at[number],
+            device_id=tuple((at[axis] + move[axis][0] + devices[axis]) % devices[axis] for axis in range(3)),
+            device_id_type=MESH,
+        ).wait()
 
     places = [(x, y, z) for x in range(tiles[0]) for y in range(tiles[1]) for z in range(tiles[2])]
     zero_row = jnp.zeros((1, slots), jnp.float32)
@@ -206,11 +233,6 @@
             gram = jnp.where(lane == pair_lane[(a, b)], value, gram)
     slots_a[pl.ds(me, 1)] = gram.reshape(1, 1, slots)
 
-    pl.semaphore_wait(barrier, total_devices - 1)
-    geom_copies = halo(geom, send_geom, recv_geom, 4)
-    everyone(0, slots_a)
-    for copy in geom_copies:
-        copy.start()
 
     wraps = tuple(n + 2 for n in tiles)
     row_of = lax.broadcasted_iota(jnp.int32, (ROWS, slots), 0)
@@ -227,48 +249,78 @@
         middle = value.astype(jnp.bfloat16).astype(jnp.float32)
         return high, middle, value - middle
 
-    def choose(values):
-        result = values[0]
-        for row, value in enumerate(values[1:], 1):
-            result = jnp.where(row_of == row, value, result)
+    def rows_in(*which):
+        result = row_of == which[0]
+        for row in which[1:]:
+            result = jnp.logical_or(result, row_of == row)
         return result
+
+    def mix(base, *choices):
+        for where, value in choices:
+            base = jnp.where(where, value, base)
+        return base
 
     one_tile = jnp.ones((ROWS, slots), jnp.float32)
     zero_tile = jnp.zeros((ROWS, slots), jnp.float32)
 
-    def broad(slot, c):
-        return jnp.broadcast_to(spots[slot[0], slot[1], slot[2], pl.ds(c, 1), :], (ROWS, slots))
+    pair_a, pair_b, pair_c, pair_d = rows_in(1, 6), rows_in(2, 4), rows_in(0, 4), rows_in(2, 5)
+    row = [row_of == number for number in range(ROWS)]
+    damp_m, damp_l = rows_in(2, 5, 6), rows_in(4, 7)
+    damp_m_i, damp_l_i = rows_in(1, 5, 7), rows_in(3, 6)
+
+    def split_rows(slot):
+        tile = spots[slot[0], slot[1], slot[2]]
+        for number, value in enumerate(pieces(tile) + pieces(tile * tile)):
+            split_ref[slot[0], slot[1], slot[2], number] = value
+
+        def take(c, *numbers):
+            return [
+                jnp.broadcast_to(split_ref[slot[0], slot[1], slot[2], number, pl.ds(c, 1), :], (ROWS, slots))
+                for number in numbers
+            ]
+
+        return take
 
     def padded(parts):
         return parts + [zero_tile] * (slots // ROWS - len(parts))
 
     def source_features(slot):
+        take = split_rows(slot)
         parts = []
         for c in range(3):
-            value = broad(slot, c)
-            high, middle, low = pieces(value)
-            square, square_middle, square_low = pieces(value * value)
+            high, middle, low, square, square_middle, square_low = take(c, 0, 1, 2, 3, 4, 5)
             parts.append(
-                choose([square, one_tile, high, square_middle, high, middle, one_tile, square_low])
+                mix(
+                    square, (pair_a, one_tile), (pair_b, high), (row[3], square_middle),
+                    (row[5], middle), (row[7], square_low),
+                )
             )
-            parts.append(choose([middle, high, low, one_tile, middle, low, zero_tile, zero_tile]))
-        high, middle, low = pieces(broad(slot, 3))
-        parts.append(choose([high, high, middle, high, low, middle, middle, low]))
+            parts.append(mix(zero_tile, (pair_c, middle), (row[1], high), (pair_d, low), (row[3], one_tile)))
+        high, middle, low = take(3, 0, 1, 2)
+        parts.append(mix(high, (damp_m, middle), (damp_l, low)))
         return jnp.concatenate(padded(parts), axis=0).astype(jnp.bfloat16)
 
     def taker_features(slot):
+        take = split_rows(slot)
         parts = []
         for c in range(3):
-            value = broad(slot, c)
-            high, middle, low = pieces(value)
-            square, square_middle, square_low = pieces(value * value)
+            high, middle, low, square, square_middle, square_low = take(c, 0, 1, 2, 3, 4, 5)
             high, middle, low = -2.0 * high, -2.0 * middle, -2.0 * low
             parts.append(
-                choose([one_tile, square, high, one_tile, middle, high, square_middle, one_tile])
+                mix(
+                    one_tile, (row[1], square), (rows_in(2, 5), high), (row[4], middle),
+                    (row[6], square_middle),
+                )
             )
-            parts.append(choose([middle, low, high, square_low, low, middle, zero_tile, zero_tile]))
-        high, middle, low = pieces(broad(slot, 3) * -THOLE_DAMP)
-        damp = choose([high, middle, high, low, high, middle, low, middle])
+            parts.append(
+                mix(
+                    zero_tile, (rows_in(0, 5), middle), (rows_in(1, 4), low), (row[2], high),
+                    (row[3], square_low),
+                )
+            )
+        value = jnp.broadcast_to(spots[slot[0], slot[1], slot[2], pl.ds(3, 1), :], (ROWS, slots))
+        high, middle, low = pieces(value * -THOLE_DAMP)
+        damp = mix(high, (damp_m_i, middle), (damp_l_i, low))
         far = jnp.concatenate(padded(parts), axis=0).astype(jnp.bfloat16)
         fade = jnp.concatenate(padded([zero_tile] * len(parts) + [damp]), axis=0).astype(jnp.bfloat16)
         return far, fade
@@ -303,7 +355,7 @@
     own_z, side_z = list(range(tiles[2])), [-1, tiles[2]]
 
     def geometry(x, y, along_x, along_y, zs):
-        nine = (along_x + 1) * 3 + along_y + 1
+        nine = (along_x + 1) * 3 + (along_y + 1)
         line = x * tiles[1] + y
         slot_x, slot_y = wrap(x + along_x, wraps[0]), wrap(y + along_y, wraps[1])
         for level in zs:
@@ -338,14 +390,20 @@
                         links[line, nine, number + 1, spot_at, part, z * slots : (z + 1) * slots] = low
 
     def geometry_near(along_x, zs):
-        def one(step, carry):
-            x = step % tiles[0]
-            y = step // tiles[0] % tiles[1]
-            to_y = step // (tiles[0] * tiles[1])
-            geometry(x, y, along_x, to_y - y, zs)
-            return carry
-
-        lax.fori_loop(0, tiles[0] * tiles[1] * tiles[1], one, 0, unroll=True)
+        for to_y in range(tiles[1]):
+            for x in range(tiles[0]):
+                for y in range(tiles[1]):
+                    if abs(to_y - y) <= 1:
+                        geometry(x, y, along_x, to_y - y, zs)
+
+    def plane_of(along_x):
+        return jnp.where(along_x > 0, tiles[0], -1)
+
+    def settle_plane(along_x, ys, zs):
+        plane = plane_of(along_x)
+        for y in ys:
+            for z in zs:
+                settle((plane, y, z), (wrap(plane, wraps[0]), y % wraps[1], z % wraps[2]))
 
     def arrive(copies, kinds_of):
         for move, copy in zip(moves, copies):
@@ -356,7 +414,7 @@
             if kind in kinds_of:
                 copy.wait()
 
-    def geometry_far():
+    def geometry_far(first, last):
         def one(step, carry):
             x = step % tiles[0]
             side = step // tiles[0] % 2
@@ -364,7 +422,7 @@
             geometry(x, side * (tiles[1] - 1), along_x, 2 * side - 1, levels)
             return carry
 
-        lax.fori_loop(0, 6 * tiles[0], one, 0, unroll=True)
+        lax.fori_loop(first * tiles[0], last * tiles[0], one, 0, unroll=True)
 
     own_x = list(range(tiles[0]))
     settle_all(own_x, near_y, own_z)
@@ -385,13 +443,26 @@
                 off_diagonal, link, 0.0
             ).astype(jnp.bfloat16)
 
+    pl.semaphore_wait(barrier, total_devices - 1)
+    geom_copies = halo(geom, send_geom, recv_geom, 4)
+    near_count = sum(1 for move in moves if move[1][0] == 0)
+    for copy in geom_copies[:near_count]:
+        copy.start()
+    everyone(0, slots_a)
+    for copy in geom_copies[near_count:]:
+        copy.start()
+    geom_parts = (geom, send_geom, recv_geom, 4)
+    arrive_x(*geom_parts, first_move)
+    settle_plane(first_x, near_y, own_z)
+    geometry_near(first_x, own_z)
     arrive(geom_copies, ("z",))
     settle_all(own_x, near_y, side_z)
     geometry_near(0, side_z)
-    arrive(geom_copies, ("x", "xz"))
-    settle_all([-1], near_y, levels)
-    settle_all([tiles[0]], near_y, levels)
-    geometry_near(-1, levels)
+    arrive_x(*geom_parts, second_move)
+    arrive(geom_copies, ("xz",))
+    settle_plane(first_x, near_y, side_z)
+    settle_plane(second_x, near_y, levels)
+    geometry_near(first_x, side_z)
 
     everyone_wait(0, slots_a)
     total = jnp.sum(slots_a[...], axis=0)
@@ -404,19 +475,17 @@
     one_copies = halo(held_one, send_one, recv_one, rows)
     for copy in one_copies:
         copy.start()
-    geometry_near(1, levels)
+    geometry_near(second_x, levels)
     arrive(geom_copies, ("far",))
     settle_all(every_x, far_y, levels)
 
     kinds = 5
 
     def weigh(held, xs, ys, zs):
-        def one(step, carry):
-            x = step * (xs[1] - xs[0] if len(xs) > 1 else 1) + xs[0]
-            x = wrap(x, wraps[0])
+        for x in xs:
             for y in ys:
                 for z in zs:
-                    slot = (x, y % wraps[1], z % wraps[2])
+                    slot = (wrap(x, wraps[0]), y % wraps[1], z % wraps[2])
                     moment = jnp.where(row_of < rows, held[slot], 0.0)
                     along = moment * turns[(0,) + slot]
                     first = jnp.sum(jnp.where(row_of < 3, along, 0.0), axis=0, keepdims=True)
@@ -437,9 +506,6 @@
                         order = order + parts[level][1:]
                     order.append(jnp.zeros((ROWS, slots), jnp.float32))
                     weights[slot] = jnp.concatenate(order, axis=0).astype(jnp.bfloat16)
-            return carry
-
-        lax.fori_loop(0, len(xs), one, 0)
 
     def products(line, visits):
         main = jnp.zeros((SPREAD, wide), jnp.float32)
@@ -559,27 +625,35 @@
             t = step * tiles[2] + z
             act(x, y, z, t, (1.0 - RELAXATION) * held[x, y, z] + scaled[t] * (fixed[t] + fields[z]))
 
-    edge_x = [-1, tiles[0]]
-
-    def first_near(held, copies):
+    def arrive_near(parts, copies):
+        arrive_x(*parts, first_move)
+        arrive_x(*parts, second_move)
+        arrive(copies, ("z", "xz"))
+
+    def first_near(held, parts, copies):
         weigh(held, own_x, near_y, own_z)
         gather([(0, own_z)], True)
-        geometry_far()
-        arrive(copies, ("x", "z", "xz"))
+        geometry_far(0, 4)
+        arrive_near(parts, copies)
         weigh(held, own_x, near_y, side_z)
-        weigh(held, edge_x, near_y, levels)
+        weigh(held, [-1, tiles[0]], near_y, levels)
+        geometry_far(4, 6)
         gather([(0, side_z), (-1, levels), (1, levels)], False)
 
-    def second_near(held, copies):
+    def second_near(held, parts, copies):
         weigh(held, own_x, near_y, own_z)
         gather([(0, own_z)], True)
-        arrive(copies, ("x", "z"))
+        arrive_x(*parts, first_move)
+        weigh(held, [plane_of(first_x)], near_y, own_z)
+        gather([(first_x, own_z)], False)
+        arrive(copies, ("z",))
         weigh(held, own_x, near_y, side_z)
-        weigh(held, edge_x, near_y, own_z)
-        gather([(0, side_z), (-1, own_z), (1, own_z)], False)
+        gather([(0, side_z)], False)
+        arrive_x(*parts, second_move)
         arrive(copies, ("xz",))
-        weigh(held, edge_x, near_y, side_z)
-        gather([(-1, side_z), (1, side_z)], False)
+        weigh(held, [plane_of(first_x)], near_y, side_z)
+        weigh(held, [plane_of(second_x)], near_y, levels)
+        gather([(first_x, side_z), (second_x, levels)], False)
 
     def sweep(held, copies, act):
         arrive(copies, ("far",))
@@ -594,7 +668,7 @@
     def first_act(x, y, z, t, value):
         held_two[x, y, z] = value
 
-    first_near(held_one, one_copies)
+    first_near(held_one, (held_one, send_one, recv_one, rows), one_copies)
     sweep(held_one, one_copies, first_act)
     two_copies = halo(held_two, send_two, recv_two, rows)
     for copy in two_copies:
@@ -603,7 +677,7 @@
     def second_act(x, y, z, t, value):
         held_one[x, y, z] = value
 
-    second_near(held_two, two_copies)
+    second_near(held_two, (held_two, send_two, recv_two, rows), two_copies)
     sweep(held_two, two_copies, second_act)
     changed = jnp.zeros((ROWS, slots), jnp.float32)
     size = jnp.zeros((ROWS, slots), jnp.float32)
@@ -664,6 +738,7 @@
                 pltpu.VMEM(wraps + (ROWS, slots), f32),
                 pltpu.VMEM((history.shape[0], count, ROWS, slots), f32),
                 pltpu.VMEM(wraps + (ROWS, slots), f32),
+                pltpu.VMEM(wraps + (6, ROWS, slots), f32),
                 pltpu.VMEM(wraps + (slots, slots), jnp.bfloat16),
                 pltpu.VMEM((lines, slots, tiles[2] * slots), jnp.bfloat16),
                 pltpu.VMEM((lines, slots, tiles[2] * slots), jnp.bfloat16),

time: 35.4 us -> 33.7 us (0.952)
  Pallas kernels: 32 us -> 30.4 us
    pallas_call x1, Pallas kernels: 32 us -> 30.4 us  [on_device(): pl.pallas_call(functools.partial(kernel, devices), out_shape=(jax.ShapeDt...]
where the time goes in v5:
time: 33.7 us; the launch traced here: 33.5 us
  Pallas kernels  30.4 us (90%)
  between operations  1.81 us (5%)
  local copies, waits for them, and re-layouts  1.31 us (4%)
    pallas_call x1, Pallas kernels, on_device(): pl.pallas_call(functools.partial(kernel, devices), out_shape=(jax.ShapeDt...  30.4 us
    unnamed x3, local copies, waits for them, and re-layouts  1.31 us

profile of v5, /device:TPU:0, one launch (start us, length us, event | category | flops | bytes accessed | tf_op | source)
XLA Modules:
  0.0 33.5 jit_solution(13197252961505263869)
XLA Ops:
  0.6 30.4 %shard_map.77 = (f32[6,1,2,2,128]{4,3,2,1,0:T(2,128)}, f32[1,128]{1,0:T(1,128)}) custom-call(f32[3,1,2,2,128]{4,3,2,1,0:T(2,128)} %frac_in.1, f32[1,2,2,128]{3,2,1,0:T(2,128)} %pol_in.1, s32[1,2,2,128]{3,2,1,0:T(2,128)} %occ_in.1, s32[1,2,2,27]{3,2,1,0:T(2,128)} %mask_in.1, f32[6,1,2,2,128]{4,3,2,1,0:T(2,128)} %perm_in.1, f32[6,6,1,2,2,128]{5,4,3,2,1,0:T(2,128)} %hist_in.1), custom_call_target="tpu_custom_call" | custom-call | tf_op jit(solution)/shard_map/pallas_call | solution.py:720
  31.0 0.0 copy-start
  31.0 1.3 %copy.10 = f32[6,1,2,2,128]{4,3,2,1,0:T(2,128)} copy(f32[6,1,2,2,128]{4,3,2,1,0:T(2,128)} %get-tuple-element.8) | data formatting | bytes 24576
  32.3 0.0 copy-done
Async XLA Ops:
  31.0 1.3 %copy-start = (f32[1,128]{1,0:T(1,128)S(1)}, f32[1,128]{1,0:T(1,128)}, u32[]{:S(2)}) copy-start(f32[1,128]{1,0:T(1,128)} %get-tuple-element.5) | copy-start | bytes 1540

commit v6 on v5

--- a/solution.py
+++ b/solution.py
@@ -561,14 +561,15 @@
 
     partials = (partial_main, partial_rest, partial_plain)
 
-    def gather(parts, start):
+    def gather(parts, start, which=None):
         def one(step, carry):
             sums = near_products(step // tiles[1], step % tiles[1], parts)
             for partial, value in zip(partials, sums):
                 partial[step] = value if start else partial[step] + value
             return carry
 
-        lax.fori_loop(0, tiles[0] * tiles[1], one, 0, unroll=True)
+        first, last = which or (0, tiles[0] * tiles[1])
+        lax.fori_loop(first, last, one, 0, unroll=True)
 
     def field_of(x, y, main, rest, plain):
         def tile(value, index):
@@ -632,13 +633,21 @@
 
     def first_near(held, parts, copies):
         weigh(held, own_x, near_y, own_z)
-        gather([(0, own_z)], True)
-        geometry_far(0, 4)
+        lines_half = (tiles[0] * tiles[1] + 1) // 2
+        halves = ((0, lines_half), (lines_half, tiles[0] * tiles[1]))
+        geometry_far(0, 1)
+        gather([(0, own_z)], True, halves[0])
+        geometry_far(1, 2)
+        gather([(0, own_z)], True, halves[1])
+        geometry_far(2, 4)
         arrive_near(parts, copies)
         weigh(held, own_x, near_y, side_z)
         weigh(held, [-1, tiles[0]], near_y, levels)
-        geometry_far(4, 6)
-        gather([(0, side_z), (-1, levels), (1, levels)], False)
+        near_parts = [(0, side_z), (-1, levels), (1, levels)]
+        geometry_far(4, 5)
+        gather(near_parts, False, halves[0])
+        geometry_far(5, 6)
+        gather(near_parts, False, halves[1])
 
     def second_near(held, parts, copies):
         weigh(held, own_x, near_y, own_z)

time: 33.7 us -> 33.8 us (level)
  no operation moved by 1% of the time
where the time goes in v6:
time: 33.8 us; the launch traced here: 33.6 us
  Pallas kernels  30.5 us (90%)
  between operations  1.81 us (5%)
  local copies, waits for them, and re-layouts  1.31 us (4%)
    pallas_call x1, Pallas kernels, on_device(): pl.pallas_call(functools.partial(kernel, devices), out_shape=(jax.ShapeDt...  30.5 us
    unnamed x3, local copies, waits for them, and re-layouts  1.31 us

profile of v6, /device:TPU:0, one launch (start us, length us, event | category | flops | bytes accessed | tf_op | source)
XLA Modules:
  0.0 33.6 jit_solution(3103724391025826434)
XLA Ops:
  0.6 30.5 %shard_map.77 = (f32[6,1,2,2,128]{4,3,2,1,0:T(2,128)}, f32[1,128]{1,0:T(1,128)}) custom-call(f32[3,1,2,2,128]{4,3,2,1,0:T(2,128)} %frac_in.1, f32[1,2,2,128]{3,2,1,0:T(2,128)} %pol_in.1, s32[1,2,2,128]{3,2,1,0:T(2,128)} %occ_in.1, s32[1,2,2,27]{3,2,1,0:T(2,128)} %mask_in.1, f32[6,1,2,2,128]{4,3,2,1,0:T(2,128)} %perm_in.1, f32[6,6,1,2,2,128]{5,4,3,2,1,0:T(2,128)} %hist_in.1), custom_call_target="tpu_custom_call" | custom-call | tf_op jit(solution)/shard_map/pallas_call | solution.py:729
  31.1 0.0 copy-start
  31.1 1.3 %copy.10 = f32[6,1,2,2,128]{4,3,2,1,0:T(2,128)} copy(f32[6,1,2,2,128]{4,3,2,1,0:T(2,128)} %get-tuple-element.8) | data formatting | bytes 24576
  32.4 0.0 copy-done
Async XLA Ops:
  31.1 1.3 %copy-start = (f32[1,128]{1,0:T(1,128)S(1)}, f32[1,128]{1,0:T(1,128)}, u32[]{:S(2)}) copy-start(f32[1,128]{1,0:T(1,128)} %get-tuple-element.5) | copy-start | bytes 1540

commit v7 on v5

--- a/solution.py
+++ b/solution.py
@@ -120,7 +120,7 @@
                     act((x, y, last))
             return carry
 
-        lax.fori_loop(0, devices[0] * devices[1], pair, 0, unroll=4)
+        lax.fori_loop(0, devices[0] * devices[1], pair, 0, unroll=8)
 
     barrier = pltpu.get_barrier_semaphore()
 
@@ -683,18 +683,20 @@
     size = jnp.zeros((ROWS, slots), jnp.float32)
     for t, (x, y, z) in enumerate(places):
         before, after = held_two[x, y, z], held_one[x, y, z]
-        for c in range(rows):
-            out_ref[c, x, y, z, :] = after[c]
         changed = changed + (after - before) * (after - before)
         size = size + after * after
-    put = pltpu.make_async_copy(out_ref, out_hbm, load_sem.at[len(loads)])
-    put.start()
 
     pair = jnp.concatenate(
         [jnp.sum(value, axis=0, keepdims=True) for value in (changed, size)], axis=1
     )
     slots_b[pl.ds(me, 1)] = pair.reshape(1, 1, 2 * slots)
     everyone(1, slots_b)
+    for x, y, z in places:
+        after = held_one[x, y, z]
+        for c in range(rows):
+            out_ref[c, x, y, z, :] = after[c]
+    put = pltpu.make_async_copy(out_ref, out_hbm, load_sem.at[len(loads)])
+    put.start()
     everyone_wait(1, slots_b)
     pair = jnp.sum(slots_b[...], axis=0)
     above = jnp.sum(pair[:, 0:slots], axis=1, keepdims=True)

time: 33.7 us -> 33.7 us (level)
  no operation moved by 1% of the time
where the time goes in v7:
time: 33.7 us; the launch traced here: 33.5 us
  Pallas kernels  30.4 us (90%)
  between operations  1.81 us (5%)
  local copies, waits for them, and re-layouts  1.31 us (4%)
    pallas_call x1, Pallas kernels, on_device(): pl.pallas_call(functools.partial(kernel, devices), out_shape=(jax.ShapeDt...  30.4 us
    unnamed x3, local copies, waits for them, and re-layouts  1.31 us

profile of v7, /device:TPU:0, one launch (start us, length us, event | category | flops | bytes accessed | tf_op | source)
XLA Modules:
  0.0 33.5 jit_solution(16381622652828137817)
XLA Ops:
  0.6 30.4 %shard_map.77 = (f32[6,1,2,2,128]{4,3,2,1,0:T(2,128)}, f32[1,128]{1,0:T(1,128)}) custom-call(f32[3,1,2,2,128]{4,3,2,1,0:T(2,128)} %frac_in.1, f32[1,2,2,128]{3,2,1,0:T(2,128)} %pol_in.1, s32[1,2,2,128]{3,2,1,0:T(2,128)} %occ_in.1, s32[1,2,2,27]{3,2,1,0:T(2,128)} %mask_in.1, f32[6,1,2,2,128]{4,3,2,1,0:T(2,128)} %perm_in.1, f32[6,6,1,2,2,128]{5,4,3,2,1,0:T(2,128)} %hist_in.1), custom_call_target="tpu_custom_call" | custom-call | tf_op jit(solution)/shard_map/pallas_call | solution.py:722
  31.0 0.0 copy-start
  31.0 1.3 %copy.10 = f32[6,1,2,2,128]{4,3,2,1,0:T(2,128)} copy(f32[6,1,2,2,128]{4,3,2,1,0:T(2,128)} %get-tuple-element.8) | data formatting | bytes 24576
  32.3 0.0 copy-done
Async XLA Ops:
  31.0 1.3 %copy-start = (f32[1,128]{1,0:T(1,128)S(1)}, f32[1,128]{1,0:T(1,128)}, u32[]{:S(2)}) copy-start(f32[1,128]{1,0:T(1,128)} %get-tuple-element.5) | copy-start | bytes 1540
